TPU v7x, 256 devices: a whole 4x4x8 slice. The times are simulated.
256 devices in a mesh: section: 2 (over core), seq: 128 (over x, z, y).
Axes of the slice: x: 4, y: 4, z: 8, core: 2. Of those that a mesh axis runs over, the one named last changes fastest.
Arguments:
- acts: bfloat16 [2, 32768, 2048], P('section', 'seq'), may hold values from -6 to 6
- in_proj: bfloat16 [2, 2048, 4640], P('section', 'seq'), may hold values from -0.125 to 0.125
- out_proj: bfloat16 [2, 2048, 2048], P('section'), may hold values from -0.125 to 0.125
- conv_weight: float32 [2, 4, 2304], P('section'), may hold values from -3 to 3
- conv_bias: float32 [2, 2304], P('section'), may hold values from -3 to 3
- dt_bias: float32 [2, 32], P('section'), may hold values from -4 to -1
- decay_rate: float32 [2, 32], P('section'), may hold values from 0.0001 to 0.5
- skip_gain: float32 [2, 32], P('section'), may hold values from -4 to 4
- level_bias: float32 [2, 256], P('section'), may hold values from -4 to 4
- norm_gain: float32 [2, 2048], P('section'), may hold values from 0.5 to 1.5
- gate_gain: float32 [2, 2048], P('section'), may hold values from 0.5 to 1.5
Outputs:
- handoff: bfloat16 [2, 32768, 2048], P('section', 'seq')
All inputs are finite; a program needn't handle non-finite values.
Results may differ from a plain program's by a relative error of at most 0.006.
Values may be sent and summed in bfloat16 or wider, within the bound.
A program may use at most 128 MiB of HBM per device.

v0:
```python
import functools
import jax
import jax.numpy as jnp
from jax import lax
from jax.experimental import pallas as pl
from jax.experimental.pallas import tpu as pltpu
from jax.sharding import PartitionSpec as P

EPS = 1e-05
MESH = pl.DeviceIdType.MESH
NX, NZ, NY = 4, 8, 4
GROUPS = NX * NZ
CA, CB = 512, 896
NP = CA + CB
ROWS = 256
F32, BF16 = jnp.float32, jnp.bfloat16


def seq_of(x, z, y):
    return (lax.rem(x + 4 * NX, NX) * NZ + lax.rem(z + 4 * NZ, NZ)) * NY + lax.rem(y + 4 * NY, NY)


def plan():
    msgs = {}
    ua, ub, un = 64 * CA * 2, 64 * CB * 2, 128 * 2048 * 2
    for d, links in ((1, {"y+": 1}), (3, {"y-": 1}), (2, {"y+": 1, "y-": 1})):
        msgs[("w", d)] = ("w", None, (0, 0, d), None, 16 * NP * 2, links)
    msgs[("P", 0)] = ("h0", 0, (0, 0, 1), None, un, {"y+": 1})
    msgs[("M", 1)] = ("h1", 0, (0, 0, -1), None, un, {"y-": 1})
    msgs[("P", 1)] = ("h1", 0, (0, 0, 1), None, un, {"y+": 1})
    msgs[("M", 0)] = ("h0", 0, (0, 0, -1), None, un, {"y-": 1})
    msgs[("P", 2)] = ("h0", -1, (0, 0, 1), ("P", 0), un, {"y+": 1})
    msgs[("M", 2)] = ("h1", 1, (0, 0, -1), ("M", 1), un, {"y-": 1})
    own = "own"
    for d, links in ((1, {"x+": 1}), (3, {"x-": 1}), (2, {"x+": 2})):
        msgs[("A1", d)] = ("a", (0, 0), (d, 0, 0), own, ua, links)
    for k in range(1, 5):
        if k < 5:
            dep = own if k == 1 else ("B1+", k - 1)
            msgs[("B1+", k)] = ("b", (0, -(k - 1)), (0, 1, 0), dep, ub, {"z+": 1})
        if k < 4:
            dep = own if k == 1 else ("B1-", k - 1)
            msgs[("B1-", k)] = ("b", (0, k - 1), (0, -1, 0), dep, ub, {"z-": 1})
    for k in range(1, 5):
        for d in range(4):
            up, down = (4, 3) if d < 2 else (3, 4)
            if k <= up:
                dep = (own if d == 0 else ("A1", d)) if k == 1 else ("A2+", d, k - 1)
                msgs[("A2+", d, k)] = ("a", (-d, -(k - 1)), (0, 1, 0), dep, ua, {"z+": 1})
            if k <= down:
                dep = (own if d == 0 else ("A1", d)) if k == 1 else ("A2-", d, k - 1)
                msgs[("A2-", d, k)] = ("a", (-d, k - 1), (0, -1, 0), dep, ua, {"z-": 1})
    offs = [0, -1, 1, -2, 2, -3, 3, -4]
    for n, o in enumerate(offs):
        dep = own if o == 0 else (("B1+", -o) if o < 0 else ("B1-", o))
        msgs[("B2+", o)] = ("b", (0, o), (1, 0, 0), dep, ub, {"x+": 1})
        msgs[("B2-", o)] = ("b", (0, o), (-1, 0, 0), dep, ub, {"x-": 1})
        if n in (1, 3, 5):
            msgs[("B2+2", o)] = ("b", (-1, o), (1, 0, 0), ("B2+", o), ub, {"x+": 1})
        else:
            msgs[("B2-2", o)] = ("b", (1, o), (-1, 0, 0), ("B2-", o), ub, {"x-": 1})
    return msgs


def schedule(msgs, rate=46.6e3, latency=1.9):
    free, arrive, order = {}, {}, []
    started = set()
    events = []

    def start(name, now):
        part, chunk, to, dep, size, links = msgs[name]
        begin = max([now] + [free.get(l, 0.0) for l in links])
        end = begin
        for l, n in links.items():
            free[l] = begin + size * n / rate
            end = max(end, free[l])
        arrive[name] = end + latency
        events.append((end + latency, len(started), name))
        started.add(name)

    for name, m in msgs.items():
        if m[3] is None:
            start(name, 0.0)
    got = set()
    while events:
        events.sort()
        now, _, name = events.pop(0)
        order.append(name)
        got.add(name)
        if all(("w", d) in got for d in (1, 2, 3)) and "own" not in got:
            got.add("own")
            order.append("own")
            for other, m in msgs.items():
                if m[3] == "own":
                    start(other, now)
        for other, m in msgs.items():
            if m[3] == name:
                start(other, now)
    return order, arrive


def gather_kernel(acts, wa_in, wb_in, gain, out, wa, wb, ablk, u, local_sems, send_sems, recv_sems):
    i = lax.axis_index("seq")
    y = lax.rem(i, NY)
    z = lax.rem(lax.div(i, NY), NZ)
    x = lax.div(i, NY * NZ)

    def there(dx, dz, dy):
        return {"seq": seq_of(x + dx, z + dz, y + dy)}

    barrier = pltpu.get_barrier_semaphore()
    near = ((1, 0, 0), (-1, 0, 0), (2, 0, 0), (0, 1, 0), (0, -1, 0), (0, 0, 1), (0, 0, -1), (0, 0, 2))
    for to in near:
        pl.semaphore_signal(barrier, inc=1, device_id=there(*to), device_id_type=MESH)

    msgs = plan()
    number = {name: n for n, name in enumerate(msgs)}
    order, _ = schedule(msgs)

    def block(rel):
        return lax.rem(y + rel + 2 * NY, NY)

    def rows_of(cx, cz):
        return pl.ds(pl.multiple_of(seq_of(x + cx, z + cz, 0) * 16, 64), 64)

    mine = pl.ds(pl.multiple_of(i * 16, 16), 16)
    local = [
        pltpu.make_async_copy(wa_in.at[y], wa.at[mine], local_sems.at[0]),
        pltpu.make_async_copy(wb_in.at[y], wb.at[mine], local_sems.at[1]),
    ]
    for copy in local:
        copy.start()
    pl.semaphore_wait(barrier, len(near))

    def remote(src, dst, n, to):
        return pltpu.make_async_remote_copy(
            src_ref=src, dst_ref=dst, send_sem=send_sems.at[n], recv_sem=recv_sems.at[n],
            device_id=there(*to), device_id_type=MESH)

    def copies(name, arriving):
        part, chunk, to, dep, _, _ = msgs[name]
        n = number[name]
        back = to if arriving else (0, 0, 0)
        if part == "w":
            d = to[2]
            if arriving:
                rows = pl.ds(pl.multiple_of(seq_of(x, z, y - d) * 16, 16), 16)
            else:
                rows = mine
            slot = lax.rem(y + d, NY)
            return [remote(wa_in.at[slot], wa.at[rows], n, to),
                    remote(wb_in.at[slot], wb.at[rows], len(msgs) + n, to)]
        if part in ("h0", "h1"):
            half = pl.ds(128 * int(part[1]), 128)
            dst = ablk.at[block(chunk - back[2]), half]
            src = acts.at[half] if chunk == 0 and not arriving else dst
            return [remote(src, dst, n, to)]
        ref = wa if part == "a" else wb
        rows = rows_of(chunk[0] - back[0], chunk[1] - back[1])
        return [remote(ref.at[rows], ref.at[rows], n, to)]

    def start(name):
        for copy in copies(name, False):
            copy.start()

    def normed(src, rel, half):
        def step(n, _):
            at = pl.multiple_of(half * 128 + n * 64, 64)
            h = src[pl.ds(at, 64), :].astype(F32)
            r = lax.rsqrt(jnp.mean(h * h, axis=1, keepdims=True) + EPS)
            to = pl.multiple_of(block(rel) * ROWS + at, 64)
            u[pl.ds(to, 64), :] = (h * r * gain[...]).astype(BF16)
            return 0

        lax.fori_loop(0, 2, step, 0)

    for name, m in msgs.items():
        if m[3] is None:
            start(name)
    normed(acts, 0, 0)
    normed(acts, 0, 1)
    halves = {("P", 0): (-1, 0), ("P", 1): (-1, 1), ("M", 1): (1, 1), ("M", 0): (1, 0), ("P", 2): (-2, 0), ("M", 2): (2, 1)}
    for name in order:
        if name == "own":
            for copy in local:
                copy.wait()
        else:
            for copy in copies(name, True):
                copy.wait_recv()
        for other, m in msgs.items():
            if m[3] == name:
                start(other)
        if name in halves:
            rel, half = halves[name]
            normed(ablk.at[block(rel)], rel, half)

    def product(n, _):
        rows = pl.ds(pl.multiple_of(n * 512, 512), 512)
        out[rows, :CA] = jnp.dot(u[rows, :], wa[...], preferred_element_type=F32).astype(BF16)
        out[rows, CA:] = jnp.dot(u[rows, :], wb[...], preferred_element_type=F32).astype(BF16)
        return 0

    lax.fori_loop(0, 2, product, 0)
    for name in msgs:
        for copy in copies(name, False):
            copy.wait_send()


def gather_project(acts, wa, wb, gain):
    count = len(plan())
    return pl.pallas_call(
        gather_kernel,
        out_shape=jax.ShapeDtypeStruct((NY * ROWS, NP), BF16),
        in_specs=[pl.BlockSpec(memory_space=pltpu.VMEM)] * 4,
        out_specs=pl.BlockSpec(memory_space=pltpu.VMEM),
        scratch_shapes=[
            pltpu.VMEM((2048, CA), BF16),
            pltpu.VMEM((2048, CB), BF16),
            pltpu.VMEM((NY, ROWS, 2048), BF16),
            pltpu.VMEM((NY * ROWS, 2048), BF16),
            pltpu.SemaphoreType.DMA((2,)),
            pltpu.SemaphoreType.DMA((count + 3,)),
            pltpu.SemaphoreType.DMA((count + 3,)),
        ],
        compiler_params=pltpu.CompilerParams(
            collective_id=0, has_side_effects=True, vmem_limit_bytes=48 * 1024 * 1024),
        name="gather_project",
    )(acts, wa, wb, gain)


def column_slices(w):
    rows = w.shape[0]
    xr = w[:, :2048].reshape(rows, NY, 512).transpose(1, 0, 2)
    bc = jnp.broadcast_to(w[None, :, 2048:2304], (NY, rows, 256))
    zg = w[:, 2304:4352].reshape(rows, NY, 512).transpose(1, 0, 2)
    dr = w[:, 4352:4384].reshape(rows, NY, 8).transpose(1, 0, 2)
    lr = w[:, 4384:4640].reshape(rows, NY, 64).transpose(1, 0, 2)
    pad = jnp.zeros((NY, rows, 56), w.dtype)
    return xr, jnp.concatenate([bc, zg, lr, dr, pad], axis=2)


HI = lax.Precision.HIGHEST


def swapped(block, apart):
    route = []
    for low in range(128):
        high = low | 1 << apart
        if high != low:
            route += [(low, high), (high, low)]
    return lax.ppermute(block, "seq", route)


def turned(block, d):
    return lax.ppermute(block, "seq", [(i, i // 4 * 4 + (i + d) % 4) for i in range(128)])


def inside(c, b, x, cum, dt, lam):
    s = jnp.dot(c, b.T, preferred_element_type=F32)
    t = lax.broadcasted_iota(jnp.int32, s.shape, 0) >= lax.broadcasted_iota(jnp.int32, s.shape, 1)
    t = t[:, :, None]
    e = jnp.where(t, jnp.exp(jnp.where(t, cum[:, None] - cum[None], 0.0)), 0.0)
    w = e * s[:, :, None] * dt[None] * lam[:, None]
    return jnp.einsum("tsh,shp->thp", w, x)


def per_device(acts, in_proj, out_proj, conv_weight, conv_bias, dt_bias, decay_rate, skip_gain, level_bias, norm_gain, gate_gain):
    i = lax.axis_index("seq")
    y = i % NY
    wa, wb = column_slices(in_proj[0])
    p = gather_project(acts[0], wa, wb, norm_gain)
    tail = lax.ppermute(p[-3:, :768], "seq", [(k, k + 4) for k in range(124)])

    def own(a, n):
        return lax.dynamic_slice_in_dim(a, y * n, n, axis=-1)

    cw = jnp.concatenate([own(conv_weight[0, :, :2048], 512), conv_weight[0, :, 2048:]], axis=1)
    cb = jnp.concatenate([own(conv_bias[0, :2048], 512), conv_bias[0, 2048:]])
    dtb, rate, skip, lb = own(dt_bias[0], 8), own(decay_rate[0], 8), own(skip_gain[0], 8), own(level_bias[0], 64)
    ext = jnp.concatenate([tail, p[:, :768]]).astype(F32)
    mixed = cb + sum(cw[k] * ext[k : k + 1024] for k in range(4))
    mixed = jax.nn.silu(mixed)
    x = mixed[:, :512].reshape(4, 256, 8, 64)
    b = mixed[:, 512:640].reshape(4, 256, 128)
    c = mixed[:, 640:].reshape(4, 256, 128)
    zg = p[:, 768:1280].astype(F32)
    dt = jax.nn.softplus(p[:, 1344:1352].astype(F32) + dtb).reshape(4, 256, 8)
    lam = jax.nn.softplus(p[:, 1280:1344].astype(F32) + lb).reshape(4, 256, 8, 8)
    cum = jnp.cumsum(-dt * rate, axis=1)
    yb = [inside(c[n], b[n], x[n], cum[n], dt[n], lam[n, :, :, 0]) for n in range(4)]
    end = cum[:, -1]
    keep = jnp.exp(end)
    st = [jnp.einsum("sn,shp->hnp", b[n], x[n] * (jnp.exp(end[n] - cum[n]) * dt[n])[..., None]) for n in range(4)]
    low = keep[1][:, None, None] * st[0] + st[1]
    high = keep[3][:, None, None] * st[2] + st[3]

    def read(n, state, level, before):
        r = jnp.einsum("tn,hnp->thp", c[n], state)
        return r * (lam[n, :, :, level] * jnp.exp(cum[n] + before))[..., None]

    zero = jnp.zeros((8,), F32)
    yb[1] += read(1, st[0], 1, zero)
    yb[3] += read(3, st[2], 1, zero)
    yb[2] += read(2, low, 2, zero)
    yb[3] += read(3, low, 2, end[2])
    before = [zero, end[0], end[0] + end[1], end[0] + end[1] + end[2]]
    blog = before[3] + end[3]
    bst = jnp.exp(end[2] + end[3])[:, None, None] * low + high
    blow = zero
    g = i // 4
    for bit in range(5):
        olog = swapped(blog, bit + 2)
        ost = swapped(bst.astype(BF16), bit + 2).astype(F32)
        upper = g >> bit & 1 == 1
        bucket = jnp.where(upper, jnp.exp(blow)[:, None, None] * ost, 0.0)
        for n in range(4):
            yb[n] += read(n, bucket, bit + 3, before[n])
        bst = jnp.where(upper, jnp.exp(blog)[:, None, None] * ost + bst, jnp.exp(olog)[:, None, None] * bst + ost)
        blow = jnp.where(upper, blow + olog, blow)
        blog = blog + olog
    yv = jnp.stack(yb).reshape(1024, 8, 64) + skip[None, :, None] * mixed[:, :512].reshape(1024, 8, 64)
    q = (yv.reshape(1024, 512) * jax.nn.silu(zg)).astype(BF16).reshape(4, 256, 512)
    got = jnp.zeros((4, 256, 512), BF16)
    got = lax.dynamic_update_index_in_dim(got, lax.dynamic_index_in_dim(q, y, 0, False), y, 0)
    for d in (1, 2, 3):
        arrived = turned(lax.dynamic_index_in_dim(q, (y + d) % 4, 0, False), d)
        got = lax.dynamic_update_index_in_dim(got, arrived, (y - d) % 4, 0)
    gated = got.transpose(1, 0, 2).reshape(256, 2048).astype(F32)
    n = (gated * lax.rsqrt(jnp.mean(gated * gated, axis=1, keepdims=True) + EPS) * gate_gain[0]).astype(BF16)
    o = (acts[0].astype(F32) + jnp.dot(n, out_proj[0], preferred_element_type=F32)).astype(BF16)
    return lax.ppermute(o, "section", [(0, 1), (1, 0)])[None]


def solution(mesh):
    two = P("section", None)
    three = P("section", None, None)
    return jax.shard_map(
        per_device,
        mesh=mesh,
        in_specs=(P("section", "seq", None), P("section", "seq", None), three, three, two, two, two, two, two, two, two),
        out_specs=P("section", "seq", None),
        check_vma=False,
    )
```

profile of v0, /device:TPU:3, one launch (start us, length us, event | category | flops | bytes accessed | tf_op | source)
XLA Modules:
  0.0 249.5 jit_solution(18244245268641376988)
XLA Ops:
  0.0 1.5 copy.180
  3.6 54.1 %gather_project.1 = bf16[1024,1408]{1,0:T(8,128)(2,1)S(1)} custom-call(bf16[256,2048]{1,0:T(8,128)(2,1)S(1)} %bitcast.429, bf16[4,16,512]{2,1,0:T(8,128)(2,1)S(1)} %bitcast.430, bf16[4,16,896]{2,1,0:T(8,128)(2,1)S(1)} %concatenate.14.wb_in, f32[1,2048]{1,0:T(1,128)S(1)} %copy-done.6), custom_call_target="tpu_custom_call" | custom-call | tf_op jit(solution)/shard_map/gather_project/pallas_call | solution.py:211
  58.4 1.9 collective-permute-start
  61.9 2.3 reduce-window.6
  67.6 1.9 copy.197
  73.9 1.8 fusion.309
  81.5 1.5 bitcast_multiply_fusion.24
  87.5 1.7 copy.209
  89.9 1.6 copy.194
  91.5 1.6 copy.222
  93.0 1.6 copy.230
  94.6 1.6 copy.232
  98.2 1.6 copy.218
  99.7 1.6 copy.220
  101.3 1.6 copy.237
  106.2 1.6 copy.233
  107.7 1.6 copy.235
  114.8 1.4 bitcast_multiply_fusion.6
  122.7 3.4 %collective-permute-start.4 = (f32[8]{0:T(128)S(1)}, f32[8]{0:T(128)S(1)}, u32[]{:S(2)}, u32[]{:S(2)}) collective-permute-start(f32[8]{0:T(128)S(1)} %get-tuple-element.18), channel_id=1, source_target_pairs={{0,8},{8,0},{1,9},{9,1},{2,10},{10,2},{3,11},{11,3},{4,12},{12,4},... | collective-permute-start | bytes 104 | tf_op jit(solution)/shard_map/ppermute | solution.py:251
  128.3 3.7 %collective-permute-start.6 = (f32[8]{0:T(128)S(1)}, f32[8]{0:T(128)S(1)}, u32[]{:S(2)}, u32[]{:S(2)}) collective-permute-start(f32[8]{0:T(128)S(1)} %get-tuple-element.120), channel_id=1, source_target_pairs={{0,16},{16,0},{1,17},{17,1},{2,18},{18,2},{3,19},{19,3},{4,20},{20... | collective-permute-start | bytes 104 | tf_op jit(solution)/shard_map/ppermute | solution.py:251
  132.0 2.6 %collective-permute-done.6 = f32[8]{0:T(128)S(1)} collective-permute-done((f32[8]{0:T(128)S(1)}, f32[8]{0:T(128)S(1)}, u32[]{:S(2)}, u32[]{:S(2)}) %collective-permute-start.6) | collective-permute-done | bytes 64 | tf_op jit(solution)/shard_map/ppermute | solution.py:251
  135.9 1.7 collective-permute-done.8
  139.2 2.0 divide_multiply_fusion
  141.2 1.7 fusion.306
  145.6 2.0 copy.189
  147.6 2.0 copy.199
  149.7 1.3 fusion.184
  155.0 2.1 copy.202
  157.0 2.0 copy.205
  160.4 1.3 fusion.312
  163.8 1.8 collective-permute-done.1
  166.5 2.5 collective-permute-start.3
  169.2 3.5 %collective-permute-done.3 = bf16[8,128,64]{1,2,0:T(8,128)(2,1)S(1)} collective-permute-done((bf16[8,128,64]{1,2,0:T(8,128)(2,1)S(1)}, bf16[8,128,64]{1,2,0:T(8,128)(2,1)S(1)}, u32[]{:S(2)}, u32[]{:S(2)}) %collective-permute-start.3) | collective-permute-done | bytes 131104 | tf_op jit(solution)/shard_map/ppermute | solution.py:251
  173.8 3.5 %collective-permute-start.5 = (bf16[8,128,64]{1,2,0:T(8,128)(2,1)S(1)}, bf16[8,128,64]{1,2,0:T(8,128)(2,1)S(1)}, u32[]{:S(2)}, u32[]{:S(2)}) collective-permute-start(bf16[8,128,64]{1,2,0:T(8,128)(2,1)S(1)} %get-tuple-element.15), channel_id=1, source_target_pairs={{0,16},{16,0},{1,17},{17,1},{2,18},{18,2},{3,19},{19,3},{4,20},{20... | collective-permute-start | bytes 393224 | tf_op jit(solution)/shard_map/ppermute | solution.py:251
  177.5 4.2 %collective-permute-done.5 = bf16[8,128,64]{1,2,0:T(8,128)(2,1)S(1)} collective-permute-done((bf16[8,128,64]{1,2,0:T(8,128)(2,1)S(1)}, bf16[8,128,64]{1,2,0:T(8,128)(2,1)S(1)}, u32[]{:S(2)}, u32[]{:S(2)}) %collective-permute-start.5) | collective-permute-done | bytes 131104 | tf_op jit(solution)/shard_map/ppermute | solution.py:251
  183.7 2.9 %collective-permute-done.7 = bf16[8,128,64]{1,2,0:T(8,128)(2,1)S(1)} collective-permute-done((bf16[8,128,64]{1,2,0:T(8,128)(2,1)S(1)}, bf16[8,128,64]{1,2,0:T(8,128)(2,1)S(1)}, u32[]{:S(2)}, u32[]{:S(2)}) %collective-permute-start.7) | collective-permute-done | bytes 131104 | tf_op jit(solution)/shard_map/ppermute | solution.py:251
  187.8 2.0 collective-permute-start.9
  190.0 3.7 %collective-permute-done.9 = bf16[8,128,64]{1,2,0:T(8,128)(2,1)S(1)} collective-permute-done((bf16[8,128,64]{1,2,0:T(8,128)(2,1)S(1)}, bf16[8,128,64]{1,2,0:T(8,128)(2,1)S(1)}, u32[]{:S(2)}, u32[]{:S(2)}) %collective-permute-start.9) | collective-permute-done | bytes 131104 | tf_op jit(solution)/shard_map/ppermute | solution.py:251
  200.0 2.8 %copy.278 = f32[4,256,8,64]{3,2,1,0:T(8,128)} copy(f32[4,256,8,64]{1,3,2,0:T(8,128)S(1)} %pad_maximum_fusion) | data formatting | bytes 4194304 | tf_op jit(solution)/shard_map/reshape | solution.py:321
  202.8 5.0 %reshape.736 = f32[1024,512]{1,0:T(8,128)} reshape(f32[4,256,8,64]{3,2,1,0:T(8,128)} %copy.278) | data formatting | bytes 4194304 | tf_op jit(solution)/shard_map/reshape | solution.py:321
  207.8 2.9 %fusion.52 = bf16[1024,512]{1,0:T(8,128)(2,1)S(1)} fusion(f32[1024,512]{1,0:T(8,128)} %reshape.736, f32[1024,768]{1,0:T(8,128)} %copy-done.7, bf16[1024,1408]{1,0:T(8,128)(2,1)S(1)} %copy-done.3, f32[512]{0:T(512)S(1)} %mul.920), kind=kLoop, calls=%fused_computation.59 | loop fusion | flops 4718592 | bytes 6293504 | tf_op jit(solution)/shard_map/convert_element_type | solution.py:322
  212.7 2.0 collective-permute-start.11
  214.8 1.5 collective-permute-start.12
  216.4 3.9 %collective-permute-done.10 = bf16[256,512]{0,1:T(8,128)(2,1)S(1)} collective-permute-done((bf16[256,512]{0,1:T(8,128)(2,1)S(1)}, bf16[256,512]{0,1:T(8,128)(2,1)S(1)}, u32[]{:S(2)}, u32[]{:S(2)}) %collective-permute-start.10) | collective-permute-done | bytes 262176 | tf_op jit(solution)/shard_map/ppermute | solution.py:255
  220.4 2.1 collective-permute-done.12
  223.2 5.7 %fusion.9 = bf16[256,2048]{1,0:T(8,128)(2,1)S(1)} fusion(bf16[256,2048]{0,1:T(8,128)(2,1)S(1)} %bitcast.439, bf16[1,2048,2048]{2,1,0:T(8,128)(2,1)} %param.13, bf16[1,256,2048]{2,1,0:T(8,128)(2,1)S(1)} %copy-done.5), kind=kOutput, calls=%fused_computation.16 | convolution fusion | flops 2149056512 | bytes 11534336 | tf_op jit(solution)/shard_map/dot_general | solution.py:330
  228.9 17.3 %collective-permute-start.13 = (bf16[256,2048]{1,0:T(8,128)(2,1)S(1)}, bf16[256,2048]{1,0:T(8,128)(2,1)S(1)}, u32[]{:S(2)}, u32[]{:S(2)}) collective-permute-start(bf16[256,2048]{1,0:T(8,128)(2,1)S(1)} %fusion.9), channel_id=1, source_target_pairs={{0,128},{128,0},{1,129},{129,1},{2,130},{130,2},{3,131},{131,3},{4... | collective-permute-start | bytes 3145736 | tf_op jit(solution)/shard_map/ppermute | solution.py:331
  246.3 2.3 collective-permute-done.13
  (317 shorter events, 70.2 us)
Async XLA Ops:
  0.0 66.4 %copy-start = (f32[1,256]{1,0:T(1,128)S(1)}, f32[1,256]{1,0:T(1,128)}, u32[]{:S(2)}) copy-start(f32[1,256]{1,0:T(1,128)} %param.19) | copy-start | bytes 3076
  1.6 58.8 %copy-start.67 = (f32[1,32]{1,0:T(1,128)S(1)}, f32[1,32]{1,0:T(1,128)}, u32[]{:S(2)}) copy-start(f32[1,32]{1,0:T(1,128)} %param.16) | copy-start | bytes 388
  1.6 58.8 %copy-start.68 = (f32[1,32]{1,0:T(1,128)S(1)}, f32[1,32]{1,0:T(1,128)}, u32[]{:S(2)}) copy-start(f32[1,32]{1,0:T(1,128)} %param.17) | copy-start | bytes 388
  3.6 62.2 %copy-start.22 = (f32[1,4,2304]{2,1,0:T(4,128)S(1)}, f32[1,4,2304]{2,1,0:T(4,128)}, u32[]{:S(2)}) copy-start(f32[1,4,2304]{2,1,0:T(4,128)} %param.14) | copy-start | bytes 110596
  57.7 9.8 %copy-start.2 = (bf16[1024,1408]{1,0:T(8,128)(2,1)}, bf16[1024,1408]{1,0:T(8,128)(2,1)S(1)}, u32[]{:S(2)}) copy-start(bf16[1024,1408]{1,0:T(8,128)(2,1)S(1)} %gather_project.1) | copy-start | bytes 8650756
  58.4 79.8 %collective-permute-start = (bf16[3,768]{1,0:T(4,128)(2,1)}, bf16[3,768]{1,0:T(4,128)(2,1)}, u32[]{:S(2)}, u32[]{:S(2)}) collective-permute-start(bf16[3,768]{1,0:T(4,128)(2,1)} %slice.365), channel_id=1, source_target_pairs={{0,4},{1,5},{2,6},{3,7},{4,8},{5,9},{6,10},{7,11},{8,12},{9,13},{1... | collective-permute-start | bytes 13832 | tf_op jit(solution)/shard_map/ppermute | solution.py:272
  65.2 56.2 %collective-permute-start.2 = (f32[8]{0:T(128)}, f32[8]{0:T(128)}, u32[]{:S(2)}, u32[]{:S(2)}) collective-permute-start(f32[8]{0:T(128)} %get-tuple-element.20), channel_id=1, source_target_pairs={{0,4},{4,0},{1,5},{5,1},{2,6},{6,2},{3,7},{7,3},{8,12},{12,8},{9,1... | collective-permute-start | bytes 104 | tf_op jit(solution)/shard_map/ppermute | solution.py:251
  65.8 9.9 %copy-start.54 = (f32[8]{0:T(128)}, f32[8]{0:T(128)S(1)}, u32[]{:S(2)}) copy-start(f32[8]{0:T(128)S(1)} %get-tuple-element.84) | copy-start | bytes 100
  65.8 9.9 %copy-start.56 = (f32[8]{0:T(128)}, f32[8]{0:T(128)S(1)}, u32[]{:S(2)}) copy-start(f32[8]{0:T(128)S(1)} %get-tuple-element.82) | copy-start | bytes 100
  69.5 8.9 %copy-start.53 = (f32[4,1,8]{2,1,0:T(1,128)S(1)}, f32[4,1,8]{2,1,0:T(1,128)}, u32[]{:S(2)}) copy-start(f32[4,1,8]{2,1,0:T(1,128)} %slice_exponential_fusion) | copy-start | bytes 388
  76.5 10.2 %copy-start.55 = (f32[8]{0:T(128)S(1)}, f32[8]{0:T(128)}, u32[]{:S(2)}) copy-start(f32[8]{0:T(128)} %copy-done.54) | copy-start | bytes 100
  76.5 10.2 %copy-start.58 = (f32[8]{0:T(128)S(1)}, f32[8]{0:T(128)}, u32[]{:S(2)}) copy-start(f32[8]{0:T(128)} %get-tuple-element.22) | copy-start | bytes 100
  87.5 31.8 %slice-start.3 = ((f32[1,2304]{1,0:T(1,128)}), f32[1,256]{1,0:T(1,128)S(1)}, s32[]{:S(2)}) async-start(f32[1,2304]{1,0:T(1,128)} %param.15), calls=%async_computation.3 | async-start | bytes 2048 | tf_op jit(solution)/shard_map/slice | solution.py:278
  87.5 50.7 %slice-start = ((bf16[1024,1408]{1,0:T(8,128)(2,1)}), bf16[1024,768]{1,0:T(8,128)(2,1)S(1)}, s32[]{:S(2)}) async-start(bf16[1024,1408]{1,0:T(8,128)(2,1)} %copy-done.2), calls=%async_computation | async-start | bytes 3145728 | tf_op jit(solution)/shard_map/slice | solution.py:280
  89.9 27.6 %copy-start.16 = (f32[256,8]{1,0:T(8,128)S(1)}, f32[256,8]{1,0:T(8,128)}, u32[]{:S(2)}) copy-start(f32[256,8]{1,0:T(8,128)} %get-tuple-element.78) | copy-start | bytes 24580
  96.8 20.6 %copy-start.17 = (f32[256,8]{1,0:T(8,128)S(1)}, f32[256,8]{1,0:T(8,128)}, u32[]{:S(2)}) copy-start(f32[256,8]{1,0:T(8,128)} %get-tuple-element.73) | copy-start | bytes 24580
  122.7 4.4 %collective-permute-start.4 = (f32[8]{0:T(128)S(1)}, f32[8]{0:T(128)S(1)}, u32[]{:S(2)}, u32[]{:S(2)}) collective-permute-start(f32[8]{0:T(128)S(1)} %get-tuple-element.18), channel_id=1, source_target_pairs={{0,8},{8,0},{1,9},{9,1},{2,10},{10,2},{3,11},{11,3},{4,12},{12,4},... | collective-permute-start | bytes 104 | tf_op jit(solution)/shard_map/ppermute | solution.py:251
  128.3 6.3 %collective-permute-start.6 = (f32[8]{0:T(128)S(1)}, f32[8]{0:T(128)S(1)}, u32[]{:S(2)}, u32[]{:S(2)}) collective-permute-start(f32[8]{0:T(128)S(1)} %get-tuple-element.120), channel_id=1, source_target_pairs={{0,16},{16,0},{1,17},{17,1},{2,18},{18,2},{3,19},{19,3},{4,20},{20... | collective-permute-start | bytes 104 | tf_op jit(solution)/shard_map/ppermute | solution.py:251
  135.2 2.4 collective-permute-start.8
  141.2 53.3 %copy-start.7 = (f32[1024,768]{1,0:T(8,128)}, f32[1024,768]{1,0:T(8,128)S(1)}, u32[]{:S(2)}) copy-start(f32[1024,768]{1,0:T(8,128)S(1)} %divide_multiply_fusion) | copy-start | bytes 9437188
  142.9 8.7 %copy-start.25 = (f32[256,8]{0,1:T(8,128)S(1)}, f32[256,8]{0,1:T(8,128)}, u32[]{:S(2)}) copy-start(f32[256,8]{0,1:T(8,128)} %copy.201) | copy-start | bytes 24580
  149.7 9.4 %copy-start.24 = (f32[256,8]{0,1:T(8,128)S(1)}, f32[256,8]{0,1:T(8,128)}, u32[]{:S(2)}) copy-start(f32[256,8]{0,1:T(8,128)} %copy.204) | copy-start | bytes 24580
  150.9 9.4 %copy-start.23 = (f32[256,8]{0,1:T(8,128)S(1)}, f32[256,8]{0,1:T(8,128)}, u32[]{:S(2)}) copy-start(f32[256,8]{0,1:T(8,128)} %copy.207) | copy-start | bytes 24580
  151.0 9.4 %copy-start.57 = (f32[8]{0:T(128)S(1)}, f32[8]{0:T(128)}, u32[]{:S(2)}) copy-start(f32[8]{0:T(128)} %get-tuple-element.80) | copy-start | bytes 100
  151.0 9.4 %copy-start.64 = (f32[8]{0:T(128)S(1)}, f32[8]{0:T(128)}, u32[]{:S(2)}) copy-start(f32[8]{0:T(128)} %get-tuple-element.113) | copy-start | bytes 100
  161.7 3.9 %collective-permute-start.1 = (bf16[8,128,64]{1,2,0:T(8,128)(2,1)S(1)}, bf16[8,128,64]{1,2,0:T(8,128)(2,1)S(1)}, u32[]{:S(2)}, u32[]{:S(2)}) collective-permute-start(bf16[8,128,64]{1,2,0:T(8,128)(2,1)S(1)} %get-tuple-element.124), channel_id=1, source_target_pairs={{0,4},{4,0},{1,5},{5,1},{2,6},{6,2},{3,7},{7,3},{8,12},{12,8},{9,1... | collective-permute-start | bytes 393224 | tf_op jit(solution)/shard_map/ppermute | solution.py:251
  162.1 10.6 %copy-start.63 = (f32[8]{0:T(128)S(1)}, f32[8]{0:T(128)}, u32[]{:S(2)}) copy-start(f32[8]{0:T(128)} %get-tuple-element.118) | copy-start | bytes 100
  165.6 8.0 %copy-start.62 = (f32[8]{0:T(128)S(1)}, f32[8]{0:T(128)}, u32[]{:S(2)}) copy-start(f32[8]{0:T(128)} %get-tuple-element.121) | copy-start | bytes 100
  165.6 8.0 %copy-start.66 = (f32[8]{0:T(128)S(1)}, f32[8]{0:T(128)}, u32[]{:S(2)}) copy-start(f32[8]{0:T(128)} %get-tuple-element.17) | copy-start | bytes 100
  166.1 15.6 %copy-start.60 = (f32[8]{0:T(128)S(1)}, f32[8]{0:T(128)}, u32[]{:S(2)}) copy-start(f32[8]{0:T(128)} %get-tuple-element.9) | copy-start | bytes 100
  166.5 6.2 %collective-permute-start.3 = (bf16[8,128,64]{1,2,0:T(8,128)(2,1)S(1)}, bf16[8,128,64]{1,2,0:T(8,128)(2,1)S(1)}, u32[]{:S(2)}, u32[]{:S(2)}) collective-permute-start(bf16[8,128,64]{1,2,0:T(8,128)(2,1)S(1)} %fusion.294), channel_id=1, source_target_pairs={{0,8},{8,0},{1,9},{9,1},{2,10},{10,2},{3,11},{11,3},{4,12},{12,4},... | collective-permute-start | bytes 393224 | tf_op jit(solution)/shard_map/ppermute | solution.py:251
  173.3 13.3 %copy-start.61 = (f32[8]{0:T(128)S(1)}, f32[8]{0:T(128)}, u32[]{:S(2)}) copy-start(f32[8]{0:T(128)} %get-tuple-element.115) | copy-start | bytes 100
  173.8 7.9 %collective-permute-start.5 = (bf16[8,128,64]{1,2,0:T(8,128)(2,1)S(1)}, bf16[8,128,64]{1,2,0:T(8,128)(2,1)S(1)}, u32[]{:S(2)}, u32[]{:S(2)}) collective-permute-start(bf16[8,128,64]{1,2,0:T(8,128)(2,1)S(1)} %get-tuple-element.15), channel_id=1, source_target_pairs={{0,16},{16,0},{1,17},{17,1},{2,18},{18,2},{3,19},{19,3},{4,20},{20... | collective-permute-start | bytes 393224 | tf_op jit(solution)/shard_map/ppermute | solution.py:251
  182.7 3.9 %collective-permute-start.7 = (bf16[8,128,64]{1,2,0:T(8,128)(2,1)S(1)}, bf16[8,128,64]{1,2,0:T(8,128)(2,1)S(1)}, u32[]{:S(2)}, u32[]{:S(2)}) collective-permute-start(bf16[8,128,64]{1,2,0:T(8,128)(2,1)S(1)} %fusion.293), channel_id=1, source_target_pairs={{0,32},{32,0},{1,33},{33,1},{2,34},{34,2},{3,35},{35,3},{4,36},{36... | collective-permute-start | bytes 393224 | tf_op jit(solution)/shard_map/ppermute | solution.py:251
  187.0 7.9 %copy-start.11 = (f32[256,512]{0,1:T(8,128)S(1)}, f32[256,512]{0,1:T(8,128)}, u32[]{:S(2)}) copy-start(f32[256,512]{0,1:T(8,128)} %copy.189) | copy-start | bytes 1572868
  187.0 7.9 %copy-start.20 = (f32[256,256]{1,0:T(8,128)S(1)}, f32[256,256]{1,0:T(8,128)}, u32[]{:S(2)}) copy-start(f32[256,256]{1,0:T(8,128)} %fusion.216) | copy-start | bytes 786436
  187.0 7.9 %copy-start.21 = (pred[256,256]{1,0:T(8,128)(4,1)S(1)}, pred[256,256]{1,0:T(8,128)(4,1)}, u32[]{:S(2)}) copy-start(pred[256,256]{1,0:T(8,128)(4,1)} %iota_compare_fusion) | copy-start | bytes 196612
  187.0 7.9 %copy-start.26 = (f32[256,8]{0,1:T(8,128)S(1)}, f32[256,8]{0,1:T(8,128)}, u32[]{:S(2)}) copy-start(f32[256,8]{0,1:T(8,128)} %copy.211) | copy-start | bytes 24580
  187.0 7.9 %copy-start.27 = (f32[256,8]{0,1:T(8,128)S(1)}, f32[256,8]{0,1:T(8,128)}, u32[]{:S(2)}) copy-start(f32[256,8]{0,1:T(8,128)} %copy.213) | copy-start | bytes 24580
  187.0 7.9 %copy-start.28 = (f32[256,8]{0,1:T(8,128)S(1)}, f32[256,8]{0,1:T(8,128)}, u32[]{:S(2)}) copy-start(f32[256,8]{0,1:T(8,128)} %copy.215) | copy-start | bytes 24580
  187.0 7.9 %copy-start.29 = (f32[256,8]{0,1:T(8,128)S(1)}, f32[256,8]{0,1:T(8,128)}, u32[]{:S(2)}) copy-start(f32[256,8]{0,1:T(8,128)} %copy.217) | copy-start | bytes 24580
  187.8 5.9 %collective-permute-start.9 = (bf16[8,128,64]{1,2,0:T(8,128)(2,1)S(1)}, bf16[8,128,64]{1,2,0:T(8,128)(2,1)S(1)}, u32[]{:S(2)}, u32[]{:S(2)}) collective-permute-start(bf16[8,128,64]{1,2,0:T(8,128)(2,1)S(1)} %fusion.197), channel_id=1, source_target_pairs={{0,64},{64,0},{1,65},{65,1},{2,66},{66,2},{3,67},{67,3},{4,68},{68... | collective-permute-start | bytes 393224 | tf_op jit(solution)/shard_map/ppermute | solution.py:251
  211.0 9.3 %collective-permute-start.10 = (bf16[256,512]{0,1:T(8,128)(2,1)S(1)}, bf16[256,512]{0,1:T(8,128)(2,1)S(1)}, u32[]{:S(2)}, u32[]{:S(2)}) collective-permute-start(bf16[256,512]{0,1:T(8,128)(2,1)S(1)} %bitcast.504), channel_id=1, source_target_pairs={{0,1},{1,2},{2,3},{3,0},{4,5},{5,6},{6,7},{7,4},{8,9},{9,10},{10,1... | collective-permute-start | bytes 786440 | tf_op jit(solution)/shard_map/ppermute | solution.py:255
  212.7 7.7 %collective-permute-start.11 = (bf16[256,512]{0,1:T(8,128)(2,1)S(1)}, bf16[256,512]{0,1:T(8,128)(2,1)S(1)}, u32[]{:S(2)}, u32[]{:S(2)}) collective-permute-start(bf16[256,512]{0,1:T(8,128)(2,1)S(1)} %bitcast.506), channel_id=1, source_target_pairs={{0,2},{1,3},{2,0},{3,1},{4,6},{5,7},{6,4},{7,5},{8,10},{9,11},{10,... | collective-permute-start | bytes 786440 | tf_op jit(solution)/shard_map/ppermute | solution.py:255
  214.8 8.4 %copy-start.5 = (bf16[1,256,2048]{2,1,0:T(8,128)(2,1)S(1)}, bf16[1,256,2048]{2,1,0:T(8,128)(2,1)}, u32[]{:S(2)}) copy-start(bf16[1,256,2048]{2,1,0:T(8,128)(2,1)} %param.11) | copy-start | bytes 3145732
  214.8 7.7 %collective-permute-start.12 = (bf16[256,512]{0,1:T(8,128)(2,1)S(1)}, bf16[256,512]{0,1:T(8,128)(2,1)S(1)}, u32[]{:S(2)}, u32[]{:S(2)}) collective-permute-start(bf16[256,512]{0,1:T(8,128)(2,1)S(1)} %bitcast.505), channel_id=1, source_target_pairs={{0,3},{1,0},{2,1},{3,2},{4,7},{5,4},{6,5},{7,6},{8,11},{9,8},{10,9... | collective-permute-start | bytes 786440 | tf_op jit(solution)/shard_map/ppermute | solution.py:255
  223.2 26.3 %copy-start.1 = (f32[1,256]{1,0:T(1,128)S(1)}, f32[1,256]{1,0:T(1,128)}, u32[]{:S(2)}) copy-start(f32[1,256]{1,0:T(1,128)} %param.19) | copy-start | bytes 3076
  228.9 19.6 %collective-permute-start.13 = (bf16[256,2048]{1,0:T(8,128)(2,1)S(1)}, bf16[256,2048]{1,0:T(8,128)(2,1)S(1)}, u32[]{:S(2)}, u32[]{:S(2)}) collective-permute-start(bf16[256,2048]{1,0:T(8,128)(2,1)S(1)} %fusion.9), channel_id=1, source_target_pairs={{0,128},{128,0},{1,129},{129,1},{2,130},{130,2},{3,131},{131,3},{4... | collective-permute-start | bytes 3145736 | tf_op jit(solution)/shard_map/ppermute | solution.py:331
  (39 other events, 106.1 us)
where the time goes:
time: 253 us; the launch traced here: 250 us
  local copies, waits for them, and re-layouts  73.9 us (29%)
  Pallas kernels  54.1 us (21%)
  starting transfers between devices  39.8 us (16%)
  waiting for transfers between devices  29.9 us (12%)
  matrix products  26.2 us (10%)
  other arithmetic  24 us (9%)
    pallas_call x1, Pallas kernels, gather_project(): pl.pallas_call(gather_kernel, out_shape=jax.ShapeDtypeStruct((NY * ROWS,...  54.1 us
    ppermute x9, waiting for transfers between devices, swapped(): return lax.ppermute(block, 'seq', route)  21.6 us
    mul x24, local copies, waits for them, and re-layouts, read(): return r * (lam[n, :, :, level] * jnp.exp(cum[n] + before))[..., None]  18.5 us
    ppermute x1, starting transfers between devices, per_device(): return lax.ppermute(o, 'section', [(0, 1), (1, 0)])[None]  17.3 us
    ppermute x9, starting transfers between devices, swapped(): return lax.ppermute(block, 'seq', route)  16.9 us
    unnamed x168, local copies, waits for them, and re-layouts  13.4 us
    unnamed x24, matrix products  8.1 us
    reshape x2, local copies, waits for them, and re-layouts, per_device(): jnp.stack(yb).reshape(1024, 8, 64)  7.8 us
  transfers between devices with their start and end apart: 14, of which 11 were waited for; matrix products, arithmetic and copies ran while one was open for 27% of the time, Pallas kernels for 0%

commit v1 on v0

--- a/solution.py
+++ b/solution.py
@@ -233,102 +233,380 @@
     xr = w[:, :2048].reshape(rows, NY, 512).transpose(1, 0, 2)
     bc = jnp.broadcast_to(w[None, :, 2048:2304], (NY, rows, 256))
     zg = w[:, 2304:4352].reshape(rows, NY, 512).transpose(1, 0, 2)
-    dr = w[:, 4352:4384].reshape(rows, NY, 8).transpose(1, 0, 2)
+    dr = jnp.repeat(w[:, 4352:4384].reshape(rows, NY, 8).transpose(1, 0, 2), 8, axis=2)
     lr = w[:, 4384:4640].reshape(rows, NY, 64).transpose(1, 0, 2)
-    pad = jnp.zeros((NY, rows, 56), w.dtype)
-    return xr, jnp.concatenate([bc, zg, lr, dr, pad], axis=2)
+    return xr, jnp.concatenate([bc, zg, lr, dr], axis=2)
 
 
 HI = lax.Precision.HIGHEST
-
-
-def swapped(block, apart):
-    route = []
-    for low in range(128):
-        high = low | 1 << apart
-        if high != low:
-            route += [(low, high), (high, low)]
-    return lax.ppermute(block, "seq", route)
-
-
-def turned(block, d):
-    return lax.ppermute(block, "seq", [(i, i // 4 * 4 + (i + d) % 4) for i in range(128)])
-
-
-def inside(c, b, x, cum, dt, lam):
-    s = jnp.dot(c, b.T, preferred_element_type=F32)
-    t = lax.broadcasted_iota(jnp.int32, s.shape, 0) >= lax.broadcasted_iota(jnp.int32, s.shape, 1)
-    t = t[:, :, None]
-    e = jnp.where(t, jnp.exp(jnp.where(t, cum[:, None] - cum[None], 0.0)), 0.0)
-    w = e * s[:, :, None] * dt[None] * lam[:, None]
-    return jnp.einsum("tsh,shp->thp", w, x)
+MID = CA + 768
+LEVELS_OUT = 5
+TABLE = (0, 16, 24, 28, 30)
+
+
+def spread(row, lanes):
+    k = lax.broadcasted_iota(jnp.int32, (128, lanes), 0)
+    c = lax.broadcasted_iota(jnp.int32, (128, lanes), 1)
+    return jnp.dot(row, (k == 64 + 8 * lax.shift_right_logical(c, 6)).astype(F32), precision=HI, preferred_element_type=F32)
+
+
+def halves_of(a, lane_low, lane_high, first):
+    return jnp.where(first, a[:, lane_low : lane_low + 1], a[:, lane_high : lane_high + 1])
+
+
+def softplus(v):
+    return jnp.maximum(v, 0.0) + jnp.log1p(jnp.exp(-jnp.abs(v)))
+
+
+def mixer_kernel(p, acts_in, wout_in, cw, cb, dtb, rate, skip, lb, gg, out,
+                 ext, xf, bcs, td, cu, yacc, near_st, eb, ee, snd1, slog, rcv1, rlog, table, rcv2, tail,
+                 qs, qr, wout, acts, acc, os, oin,
+                 in_sems, ssem, rsem, lsend, lrecv, tsem, qsend, qrecv, osend, orecv, dsem):
+    i = lax.axis_index("seq")
+    y = lax.rem(i, NY)
+    g = lax.div(i, NY)
+    s = lax.axis_index("section")
+
+    def group(n):
+        return {"seq": n * NY + y}
+
+    def beside(n):
+        return {"seq": g * NY + lax.rem(y + n, NY)}
+
+    def wrap(n):
+        return lax.rem(n, GROUPS)
+
+    def remote(src, dst, send, recv, to):
+        return pltpu.make_async_remote_copy(
+            src_ref=src, dst_ref=dst, send_sem=send, recv_sem=recv, device_id=to, device_id_type=MESH)
+
+    barrier = pltpu.get_barrier_semaphore()
+
+    def greet(d, _):
+        pl.semaphore_signal(barrier, inc=1, device_id=group(wrap(g + d)), device_id_type=MESH)
+        return 0
+
+    lax.fori_loop(1, GROUPS, greet, 0)
+    for d in (1, 2, 3):
+        pl.semaphore_signal(barrier, inc=1, device_id=beside(d), device_id_type=MESH)
+    pl.semaphore_signal(barrier, inc=1, device_id={"section": 1 - s}, device_id_type=MESH)
+    loads = [pltpu.make_async_copy(acts_in, acts, in_sems.at[0]), pltpu.make_async_copy(wout_in, wout, in_sems.at[1])]
+    for copy in loads:
+        copy.start()
+
+    def picked(v, hit):
+        rows = jnp.broadcast_to(v[...], (8, v.shape[1]))
+        return jnp.dot(rows, hit.astype(F32), precision=HI, preferred_element_type=F32)[:1]
+
+    def two(rows, lanes):
+        return (lax.broadcasted_iota(jnp.int32, (rows, lanes), 0), lax.broadcasted_iota(jnp.int32, (rows, lanes), 1))
+
+    k, c = two(32, 128)
+    of_head = (c >= 64) & (k == 8 * y + lax.shift_right_logical(c - 64, 3))
+    k2, c2 = two(256, 128)
+    bias = picked(dtb, of_head) + picked(lb, (c2 < 64) & (k2 == 64 * y + c2))
+    rates = picked(rate, of_head)
+    k3, c3 = two(32, 512)
+    skips = picked(skip, k3 == 8 * y + lax.shift_right_logical(c3, 6))
+
+    low_tri = (lax.broadcasted_iota(jnp.int32, (ROWS, ROWS), 1) <= lax.broadcasted_iota(jnp.int32, (ROWS, ROWS), 0)).astype(BF16)
+    for b in range(4):
+        rows = slice(b * ROWS, (b + 1) * ROWS)
+        t = softplus(p[rows, MID:].astype(F32) + bias)
+        td[rows, :] = t
+        left = -t * rates
+        total = jnp.zeros((ROWS, 128), F32)
+        for _ in range(3):
+            piece = left.astype(BF16)
+            total = total + jnp.dot(low_tri, piece, preferred_element_type=F32)
+            left = left - piece.astype(F32)
+        cu[rows, :] = total
+        eb[b : b + 1, :] = total[ROWS - 1 :, :]
+    eb[4:, :] = jnp.zeros((4, 128), F32)
+    ends = eb[...]
+    ee[...] = jnp.exp(spread(ends, 512))
+    slog[...] = jnp.broadcast_to(jnp.sum(ends, axis=0, keepdims=True), (8, 128))
+
+    pl.semaphore_wait(barrier, GROUPS - 1 + 3 + 1)
+    back = remote(p.at[pl.ds(1008, 16), pl.ds(0, 768)], tail, tsem.at[0], tsem.at[1], group(wrap(g + 1)))
+    back.start()
+
+    for n in range(4):
+        ext[8 + n * ROWS : 8 + (n + 1) * ROWS, :] = p[n * ROWS : (n + 1) * ROWS, :768].astype(F32)
+    own = pl.ds(pl.multiple_of(y * 512, 512), 512)
+    tx = [cw[k : k + 1, own] for k in range(4)]
+    tb = [cw[k : k + 1, 2048:] for k in range(4)]
+    bx, bb = cb[:, own], cb[:, 2048:]
+
+    def convolved(n):
+        at = n * 128
+        v = bx
+        for k in range(4):
+            v = v + tx[k] * ext[at + 5 + k : at + 133 + k, :512]
+        xf[at : at + 128, :] = jax.nn.silu(v)
+        v = bb
+        for k in range(4):
+            v = v + tb[k] * ext[at + 5 + k : at + 133 + k, 512:]
+        bcs[at : at + 128, :] = jax.nn.silu(v).astype(BF16)
+
+    for n in range(1, 8):
+        convolved(n)
+    back.wait_recv()
+    before = tail[...].astype(F32)
+    ext[0:8, :] = jnp.where(g > 0, before[8:, :], 0.0)
+    convolved(0)
+
+    first = lax.broadcasted_iota(jnp.int32, (1, 128), 1) < 64
+
+    def state(b):
+        rows = slice(b * ROWS, (b + 1) * ROWS)
+        tl = jnp.exp(ends[b : b + 1, :] - cu[rows, :]) * td[rows, :]
+        parts = []
+        for h in range(4):
+            parts.append((xf[rows, 128 * h : 128 * h + 128] * halves_of(tl, 64 + 16 * h, 72 + 16 * h, first)).astype(BF16))
+        xt = jnp.concatenate(parts, axis=1)
+        return lax.dot_general(bcs[rows, :128], xt, (((0,), (0,)), ((), ())), preferred_element_type=F32)
+
+    st = state(0)
+    near_st[0] = st.astype(BF16)
+    st = ee[1:2, :] * st + state(1)
+    near_st[1] = st.astype(BF16)
+    other = state(2)
+    near_st[2] = other.astype(BF16)
+    st = ee[2:3, :] * ee[3:4, :] * st + ee[3:4, :] * other + state(3)
+    st = st.astype(BF16)
+    for n in range(GROUPS):
+        ct, nt = n // 8, n % 8
+        snd1[n] = st[16 * nt : 16 * nt + 16, 128 * ct : 128 * ct + 128]
+
+    def first_send(d, _):
+        to = wrap(g + d)
+        remote(snd1.at[to], rcv1.at[g], ssem.at[0], rsem.at[0], group(to)).start()
+        remote(slog, rlog.at[g], ssem.at[1], rsem.at[1], group(to)).start()
+        return 0
+
+    lax.fori_loop(1, GROUPS, first_send, 0)
+    rcv1[g] = snd1[g]
+    rlog[g] = slog[...]
+
+    def inside(b, _):
+        base = pl.multiple_of(b * ROWS, ROWS)
+        every = pl.ds(base, ROWS)
+        cum_t = jnp.transpose(cu[every, :])
+        dt_t = jnp.transpose(td[every, :])
+        for r in range(2):
+            rows = pl.ds(pl.multiple_of(base + 128 * r, 128), 128)
+            wide = 128 * (r + 1)
+            seen = pl.ds(base, wide)
+            scores = lax.dot_general(bcs[rows, 128:], bcs[seen, :128], (((1,), (1,)), ((), ())), preferred_element_type=F32)
+            ti, si = two(128, wide)
+            causal = si <= ti + 128 * r
+            cum, lam = cu[rows, :], td[rows, :]
+            for h in range(4):
+                xp = xf[seen, 128 * h : 128 * h + 128].astype(BF16)
+                got = []
+                for e in (2 * h, 2 * h + 1):
+                    lane = 64 + 8 * e
+                    differ = jnp.where(causal, cum[:, lane : lane + 1] - cum_t[lane : lane + 1, :wide], -1e30)
+                    w = scores * jnp.exp(differ) * dt_t[lane : lane + 1, :wide]
+                    got.append(jnp.dot(w.astype(BF16), xp, preferred_element_type=F32))
+                val = jnp.where(first, got[0], got[1]) * halves_of(lam, 16 * h, 16 * h + 8, first)
+                cols = slice(128 * h, 128 * h + 128)
+                yacc[rows, cols] = val + skips[:, cols] * xf[rows, cols]
+        return 0
+
+    lax.fori_loop(0, 4, inside, 0)
+
+    remote(rcv1.at[pl.ds(0, GROUPS - 1)], rcv1.at[pl.ds(0, GROUPS - 1)], ssem.at[0], rsem.at[0], group(g)).wait_recv()
+    remote(rlog.at[pl.ds(0, GROUPS - 1)], rlog.at[pl.ds(0, GROUPS - 1)], ssem.at[1], rsem.at[1], group(g)).wait_recv()
+    logs = rlog[:, 0, :]
+    wide_logs = spread(logs, 512)
+    ct = lax.div(g, 8)
+    mine = jnp.zeros((GROUPS, 128), F32)
+    for n in range(4):
+        mine = jnp.where(ct == n, wide_logs[:, 128 * n : 128 * n + 128], mine)
+    level = [rcv1[n].astype(F32) for n in range(GROUPS)]
+    ends_of = [mine[n : n + 1, :] for n in range(GROUPS)]
+    for l in range(LEVELS_OUT):
+        for n in range(0, len(level), 2):
+            table[TABLE[l] + n // 2] = level[n].astype(BF16)
+        level = [jnp.exp(ends_of[n + 1]) * level[n] + level[n + 1] for n in range(0, len(level), 2)]
+        ends_of = [ends_of[n] + ends_of[n + 1] for n in range(0, len(ends_of), 2)]
+
+    def second_send(d, _):
+        to = wrap(g + d)
+        for l in range(LEVELS_OUT):
+            up = lax.div(to, 2**l)
+
+            @pl.when(lax.rem(up, 2) == 1)
+            def _():
+                remote(table.at[TABLE[l] + lax.div(up, 2)], rcv2.at[l, g], lsend.at[l], lrecv.at[l], group(to)).start()
+
+        return 0
+
+    lax.fori_loop(1, GROUPS, second_send, 0)
+    bits = [lax.rem(lax.div(g, 2**l), 2) for l in range(LEVELS_OUT)]
+
+    lane8 = lax.broadcasted_iota(jnp.int32, (1, 128), 1) & 7
+
+    def read(b, rows, bucket, scale, lev):
+        r = jnp.dot(bcs[rows, 128:], bucket, preferred_element_type=F32)
+        for h in range(4):
+            cols = slice(128 * h, 128 * h + 128)
+            yacc[rows, cols] += r[:, cols] * halves_of(scale, 16 * h + lev, 16 * h + 8 + lev, first)
+
+    def scales(rows, add):
+        return pltpu.roll(jnp.exp(cu[rows, :] + add), 64, 1) * td[rows, :]
+
+    zero = jnp.zeros((1, 128), F32)
+    block = [pl.ds(b * ROWS, ROWS) for b in range(4)]
+    read(1, block[1], near_st[0], scales(block[1], zero), 1)
+    read(2, block[2], near_st[1], scales(block[2], zero), 2)
+    sc = scales(block[3], jnp.where(lane8 == 2, ends[2:3, :], 0.0))
+    read(3, block[3], near_st[2], sc, 1)
+    read(3, block[3], near_st[1], sc, 2)
+
+    row_of = lax.broadcasted_iota(jnp.int32, (GROUPS, 1), 0)
+    outer = zero
+    for l in range(LEVELS_OUT):
+        start = lax.div(g, 2**l) * 2**l
+        summed = jnp.sum(jnp.where((row_of >= start) & (row_of < g), logs, 0.0), axis=0, keepdims=True)
+        outer = jnp.where(lane8 == l + 3, summed, outer)
+    run = zero
+    for b in range(4):
+        eb[4 + b : 5 + b, :] = run + outer
+        run = run + ends[b : b + 1, :]
+
+    for l in range(LEVELS_OUT):
+        @pl.when(bits[l] == 1)
+        def _():
+            remote(rcv2.at[l, pl.ds(0, GROUPS - 1)], rcv2.at[l, pl.ds(0, GROUPS - 1)], lsend.at[l], lrecv.at[l], group(g)).wait_recv()
+            rcv2[l, g] = table[TABLE[l] + lax.div(g, 2 ** (l + 1))]
+
+        @pl.when(bits[l] == 0)
+        def _():
+            rcv2[l] = jnp.zeros((GROUPS, 16, 128), BF16)
+
+    def finish(n, _):
+        b = lax.rem(y + n, NY)
+        base = pl.multiple_of(b * ROWS, ROWS)
+        for half in range(2):
+            rows = pl.ds(pl.multiple_of(base + 128 * half, 128), 128)
+            scale = scales(rows, eb[pl.ds(4 + b, 1), :])
+            c = bcs[rows, 128:]
+            for h in range(0, 4, 2):
+                vals = [yacc[rows, 128 * (h + e) : 128 * (h + e) + 128] for e in range(2)]
+                for l in range(LEVELS_OUT):
+                    pair = [rcv2[l, 8 * (h + e) : 8 * (h + e) + 8].reshape(128, 128) for e in range(2)]
+                    r = jnp.dot(c, jnp.concatenate(pair, axis=1), preferred_element_type=F32)
+                    for e in range(2):
+                        lane = 16 * (h + e) + l + 3
+                        vals[e] = vals[e] + r[:, 128 * e : 128 * e + 128] * halves_of(scale, lane, lane + 8, first)
+                for e in range(2):
+                    cols = slice(128 * (h + e), 128 * (h + e) + 128)
+                    zg = p[rows, 768 + 128 * (h + e) : 896 + 128 * (h + e)].astype(F32)
+                    qs[b, 128 * half : 128 * half + 128, cols] = (vals[e] * jax.nn.silu(zg)).astype(BF16)
+
+        @pl.when(n < 4)
+        def _():
+            remote(qs.at[b], qr.at[y], qsend.at[n], qrecv.at[n], beside(n)).start()
+
+        return 0
+
+    lax.fori_loop(1, 5, finish, 0)
+    qr[y] = qs[y]
+    for copy in loads:
+        copy.wait()
+
+    squares = jnp.zeros((ROWS, 1), F32)
+    for at, n in enumerate((0, 1, 3, 2)):
+        src = lax.rem(y + NY - n, NY)
+        if n:
+            remote(qs.at[0], qr.at[src], qsend.at[n], qrecv.at[n], beside(n)).wait_recv()
+        v = qr[src].astype(F32)
+        squares = squares + jnp.sum(v * v, axis=1, keepdims=True)
+        lanes = pl.ds(pl.multiple_of(src * 512, 512), 512)
+        v = (v * gg[:, lanes]).astype(BF16)
+        for t in range(4):
+            cols = slice(512 * t, 512 * t + 512)
+            part = jnp.dot(v, wout[lanes, cols], preferred_element_type=F32)
+            acc[:, cols] = part if at == 0 else acc[:, cols] + part
+    r = lax.rsqrt(squares * (1.0 / 2048.0) + EPS)
+    sends = []
+    for t in range(4):
+        cols = slice(512 * t, 512 * t + 512)
+        os[t] = (acts[:, cols].astype(F32) + r * acc[:, cols]).astype(BF16)
+        sends.append(remote(os.at[t], oin.at[t], osend.at[t], orecv.at[t], {"section": 1 - s}))
+        sends[-1].start()
+    stores = []
+    for t in range(4):
+        sends[t].wait_recv()
+        stores.append(pltpu.make_async_copy(oin.at[t], out.at[:, pl.ds(512 * t, 512)], dsem.at[t]))
+        stores[-1].start()
+    back.wait_send()
+    remote(rcv1.at[pl.ds(0, GROUPS - 1)], rcv1.at[pl.ds(0, GROUPS - 1)], ssem.at[0], rsem.at[0], group(g)).wait_send()
+    remote(rlog.at[pl.ds(0, GROUPS - 1)], rlog.at[pl.ds(0, GROUPS - 1)], ssem.at[1], rsem.at[1], group(g)).wait_send()
+    for l in range(LEVELS_OUT):
+        for bit in range(2):
+            @pl.when(bits[l] == bit)
+            def _():
+                some = rcv2.at[l, pl.ds(0, 16 - bit)]
+                remote(some, some, lsend.at[l], lrecv.at[l], group(g)).wait_send()
+    for n in (1, 2, 3):
+        remote(qs.at[0], qr.at[y], qsend.at[n], qrecv.at[n], beside(n)).wait_send()
+    for copy in sends:
+        copy.wait_send()
+    for copy in stores:
+        copy.wait()
+
+
+def mix(p, acts, wout, *params):
+    vmem = pl.BlockSpec(memory_space=pltpu.VMEM)
+    anywhere = pl.BlockSpec(memory_space=pl.ANY)
+    n = NY * ROWS
+    dma = pltpu.SemaphoreType.DMA
+    return pl.pallas_call(
+        mixer_kernel,
+        out_shape=jax.ShapeDtypeStruct((ROWS, 2048), BF16),
+        in_specs=[vmem, anywhere, anywhere] + [vmem] * len(params),
+        out_specs=anywhere,
+        scratch_shapes=[
+            pltpu.VMEM((n + 8, 768), F32),
+            pltpu.VMEM((n, 512), F32),
+            pltpu.VMEM((n, 256), BF16),
+            pltpu.VMEM((n, 128), F32),
+            pltpu.VMEM((n, 128), F32),
+            pltpu.VMEM((n, 512), F32),
+            pltpu.VMEM((3, 128, 512), BF16),
+            pltpu.VMEM((8, 128), F32),
+            pltpu.VMEM((8, 512), F32),
+            pltpu.VMEM((GROUPS, 16, 128), BF16),
+            pltpu.VMEM((8, 128), F32),
+            pltpu.VMEM((GROUPS, 16, 128), BF16),
+            pltpu.VMEM((GROUPS, 8, 128), F32),
+            pltpu.VMEM((31, 16, 128), BF16),
+            pltpu.VMEM((LEVELS_OUT, GROUPS, 16, 128), BF16),
+            pltpu.VMEM((16, 768), BF16),
+            pltpu.VMEM((NY, ROWS, 512), BF16),
+            pltpu.VMEM((NY, ROWS, 512), BF16),
+            pltpu.VMEM((2048, 2048), BF16),
+            pltpu.VMEM((ROWS, 2048), BF16),
+            pltpu.VMEM((ROWS, 2048), F32),
+            pltpu.VMEM((4, ROWS, 512), BF16),
+            pltpu.VMEM((4, ROWS, 512), BF16),
+            dma((2,)), dma((2,)), dma((2,)), dma((5,)), dma((5,)), dma((2,)), dma((4,)), dma((4,)), dma((4,)), dma((4,)), dma((4,)),
+        ],
+        compiler_params=pltpu.CompilerParams(
+            collective_id=1, has_side_effects=True, vmem_limit_bytes=52 * 1024 * 1024),
+        name="mix",
+    )(p, acts, wout, *params)
 
 
 def per_device(acts, in_proj, out_proj, conv_weight, conv_bias, dt_bias, decay_rate, skip_gain, level_bias, norm_gain, gate_gain):
-    i = lax.axis_index("seq")
-    y = i % NY
     wa, wb = column_slices(in_proj[0])
     p = gather_project(acts[0], wa, wb, norm_gain)
-    tail = lax.ppermute(p[-3:, :768], "seq", [(k, k + 4) for k in range(124)])
-
-    def own(a, n):
-        return lax.dynamic_slice_in_dim(a, y * n, n, axis=-1)
-
-    cw = jnp.concatenate([own(conv_weight[0, :, :2048], 512), conv_weight[0, :, 2048:]], axis=1)
-    cb = jnp.concatenate([own(conv_bias[0, :2048], 512), conv_bias[0, 2048:]])
-    dtb, rate, skip, lb = own(dt_bias[0], 8), own(decay_rate[0], 8), own(skip_gain[0], 8), own(level_bias[0], 64)
-    ext = jnp.concatenate([tail, p[:, :768]]).astype(F32)
-    mixed = cb + sum(cw[k] * ext[k : k + 1024] for k in range(4))
-    mixed = jax.nn.silu(mixed)
-    x = mixed[:, :512].reshape(4, 256, 8, 64)
-    b = mixed[:, 512:640].reshape(4, 256, 128)
-    c = mixed[:, 640:].reshape(4, 256, 128)
-    zg = p[:, 768:1280].astype(F32)
-    dt = jax.nn.softplus(p[:, 1344:1352].astype(F32) + dtb).reshape(4, 256, 8)
-    lam = jax.nn.softplus(p[:, 1280:1344].astype(F32) + lb).reshape(4, 256, 8, 8)
-    cum = jnp.cumsum(-dt * rate, axis=1)
-    yb = [inside(c[n], b[n], x[n], cum[n], dt[n], lam[n, :, :, 0]) for n in range(4)]
-    end = cum[:, -1]
-    keep = jnp.exp(end)
-    st = [jnp.einsum("sn,shp->hnp", b[n], x[n] * (jnp.exp(end[n] - cum[n]) * dt[n])[..., None]) for n in range(4)]
-    low = keep[1][:, None, None] * st[0] + st[1]
-    high = keep[3][:, None, None] * st[2] + st[3]
-
-    def read(n, state, level, before):
-        r = jnp.einsum("tn,hnp->thp", c[n], state)
-        return r * (lam[n, :, :, level] * jnp.exp(cum[n] + before))[..., None]
-
-    zero = jnp.zeros((8,), F32)
-    yb[1] += read(1, st[0], 1, zero)
-    yb[3] += read(3, st[2], 1, zero)
-    yb[2] += read(2, low, 2, zero)
-    yb[3] += read(3, low, 2, end[2])
-    before = [zero, end[0], end[0] + end[1], end[0] + end[1] + end[2]]
-    blog = before[3] + end[3]
-    bst = jnp.exp(end[2] + end[3])[:, None, None] * low + high
-    blow = zero
-    g = i // 4
-    for bit in range(5):
-        olog = swapped(blog, bit + 2)
-        ost = swapped(bst.astype(BF16), bit + 2).astype(F32)
-        upper = g >> bit & 1 == 1
-        bucket = jnp.where(upper, jnp.exp(blow)[:, None, None] * ost, 0.0)
-        for n in range(4):
-            yb[n] += read(n, bucket, bit + 3, before[n])
-        bst = jnp.where(upper, jnp.exp(blog)[:, None, None] * ost + bst, jnp.exp(olog)[:, None, None] * bst + ost)
-        blow = jnp.where(upper, blow + olog, blow)
-        blog = blog + olog
-    yv = jnp.stack(yb).reshape(1024, 8, 64) + skip[None, :, None] * mixed[:, :512].reshape(1024, 8, 64)
-    q = (yv.reshape(1024, 512) * jax.nn.silu(zg)).astype(BF16).reshape(4, 256, 512)
-    got = jnp.zeros((4, 256, 512), BF16)
-    got = lax.dynamic_update_index_in_dim(got, lax.dynamic_index_in_dim(q, y, 0, False), y, 0)
-    for d in (1, 2, 3):
-        arrived = turned(lax.dynamic_index_in_dim(q, (y + d) % 4, 0, False), d)
-        got = lax.dynamic_update_index_in_dim(got, arrived, (y - d) % 4, 0)
-    gated = got.transpose(1, 0, 2).reshape(256, 2048).astype(F32)
-    n = (gated * lax.rsqrt(jnp.mean(gated * gated, axis=1, keepdims=True) + EPS) * gate_gain[0]).astype(BF16)
-    o = (acts[0].astype(F32) + jnp.dot(n, out_proj[0], preferred_element_type=F32)).astype(BF16)
-    return lax.ppermute(o, "section", [(0, 1), (1, 0)])[None]
+    o = mix(p, acts[0], out_proj[0], conv_weight[0], conv_bias, dt_bias, decay_rate, skip_gain, level_bias, gate_gain)
+    return o[None]
 
 
 def solution(mesh):

time: 253 us -> 111 us (0.44); the launches traced: 250 us -> 111 us
  local copies, waits for them, and re-layouts: 73.9 us -> 5.34 us
  Pallas kernels: 54.1 us -> 106 us
  starting transfers between devices: 39.8 us -> 0 us
  waiting for transfers between devices: 29.9 us -> 0 us
  matrix products: 26.2 us -> 0 us
  other arithmetic: 24 us -> 0.08 us
    pallas_call x0 -> x1, Pallas kernels: none -> 51.3 us  [mix(): pl.pallas_call(mixer_kernel, out_shape=jax.ShapeDtypeStruct((ROWS, 2048),...]
    ppermute x14 -> x0, starting transfers between devices: 39.8 us -> none  [the longest x1 17.3 us: per_device(): return lax.ppermute(o, 'section', [(0, 1), (1, 0)])[None]]
    ppermute x14 -> x0, waiting for transfers between devices: 29.9 us -> none  [the longest x9 21.6 us: swapped(): return lax.ppermute(block, 'seq', route)]
    mul x33 -> x0, local copies, waits for them, and re-layouts: 22 us -> none  [the longest x24 18.5 us: read(): return r * (lam[n, :, :, level] * jnp.exp(cum[n] + before))[..., None]]
    dot_general x13 -> x0, matrix products: 18.1 us -> none  [the longest x1 5.73 us: per_device(): jnp.dot(n, out_proj[0], preferred_element_type=F32)]
    slice x24 -> x0, local copies, waits for them, and re-layouts: 17.7 us -> none  [the longest x3 6.12 us: per_device(): x[n] * (jnp.exp(end[n] - cum[n]) * dt[n])[..., None]]
    reshape x5 -> x2, local copies, waits for them, and re-layouts: 9.01 us -> 0.1 us  [column_slices(): jnp.repeat(w[:, 4352:4384].reshape(rows, NY, 8).transpose(1, 0, 2), 8, ax...]
    unnamed x168 -> x22, local copies, waits for them, and re-layouts: 13.4 us -> 4.6 us
  transfers between devices with their start and end apart: 14 -> 0, of which waited for: 11 -> 0; matrix products, arithmetic and copies ran while one was open for 27% -> 0% of each run, Pallas kernels for 0% -> 0%
where the time goes in v1:
time: 111 us
  Pallas kernels  106 us (95%)
  local copies, waits for them, and re-layouts  5.34 us (5%)
    pallas_call x1, Pallas kernels, gather_project(): pl.pallas_call(gather_kernel, out_shape=jax.ShapeDtypeStruct((NY * ROWS,...  54.3 us
    pallas_call x1, Pallas kernels, mix(): pl.pallas_call(mixer_kernel, out_shape=jax.ShapeDtypeStruct((ROWS, 2048),...  51.3 us
    unnamed x22, local copies, waits for them, and re-layouts  4.6 us

profile of v1, /device:TPU:3, one launch (start us, length us, event | category | flops | bytes accessed | tf_op | source)
XLA Modules:
  0.0 111.1 jit_solution(397288007403079775)
XLA Ops:
  0.0 1.4 %copy.13 = bf16[1,16,4640]{1,2,0:T(8,128)(2,1)S(1)} copy(bf16[1,16,4640]{2,1,0:T(8,128)(2,1)} %param.12) | data formatting | bytes 296960 | tf_op args[1]
  1.5 0.1 copy.21
  1.6 0.1 fusion.1
  1.7 0.0 copy-start.1
  1.7 0.0 copy-start.4
  1.7 0.2 copy.18
  1.9 0.2 copy.15
  2.1 0.1 copy.16
  2.1 0.1 copy.20
  2.3 0.1 pad_maximum_fusion.wb_in
  2.3 0.6 copy-done.1
  2.9 0.0 copy-done.4
  2.9 0.0 copy-start.2
  2.9 0.0 copy-start.3
  2.9 0.0 copy-start.5
  2.9 0.0 copy-start.6
  2.9 0.0 copy-start.7
  2.9 0.0 copy-start.8
  2.9 0.0 copy-start.9
  3.0 54.3 %gather_project.1.p = bf16[1024,1408]{1,0:T(8,128)(2,1)S(1)} custom-call(bf16[256,2048]{1,0:T(8,128)(2,1)S(1)} %bitcast.19, bf16[4,16,512]{2,1,0:T(8,128)(2,1)S(1)} %bitcast.20, bf16[4,16,896]{2,1,0:T(8,128)(2,1)S(1)} %pad_maximum_fusion.wb_in, f32[1,2048]{1,0:T(1,128)S(1)} %copy-done.4), custom_call_target="tpu_custom_call" | custom-call | tf_op jit(solution)/shard_map/gather_project/pallas_call | solution.py:211
  57.3 0.0 copy-start
  57.3 1.6 %copy-done = bf16[1024,1408]{1,0:T(8,128)(2,1)} copy-done((bf16[1024,1408]{1,0:T(8,128)(2,1)}, bf16[1024,1408]{1,0:T(8,128)(2,1)S(1)}, u32[]{:S(2)}) %copy-start) | copy-done | bytes 2883608
  58.8 0.0 copy-done.2
  58.9 0.0 copy-done.3
  58.9 0.0 copy-done.5
  58.9 0.0 copy-done.6
  58.9 0.0 copy-done.7
  58.9 0.0 copy-done.8
  58.9 0.0 copy-done.9
  58.9 51.3 %mix.1 = bf16[256,2048]{1,0:T(8,128)(2,1)S(1)} custom-call(bf16[1024,1408]{1,0:T(8,128)(2,1)} %copy-done, bf16[256,2048]{1,0:T(8,128)(2,1)} %bitcast.18, bf16[2048,2048]{1,0:T(8,128)(2,1)} %bitcast.22, f32[4,2304]{1,0:T(4,128)S(1)} %bitcast.21, f32[1,2304]{1,0:T(1,128)S(1)} %copy-done.3, f32[1,32]{1,0:T(1,128)S(1)} %copy-done.7, f32[1,32]{1,0:T(1,128)S(1)} %copy-done.8, ...), custom_call_target="tpu_custom_call" | custom-call | tf_op jit(solution)/shard_map/mix/pallas_call | solution.py:568
  110.2 1.0 copy.29
  (4 shorter events, 0.0 us)
Async XLA Ops:
  1.7 1.2 %copy-start.1 = (bf16[1,256,2048]{2,1,0:T(8,128)(2,1)S(1)}, bf16[1,256,2048]{2,1,0:T(8,128)(2,1)}, u32[]{:S(2)}) copy-start(bf16[1,256,2048]{2,1,0:T(8,128)(2,1)} %param.11) | copy-start | bytes 3145732
  1.7 1.2 %copy-start.4 = (f32[1,2048]{1,0:T(1,128)S(1)}, f32[1,2048]{1,0:T(1,128)}, u32[]{:S(2)}) copy-start(f32[1,2048]{1,0:T(1,128)} %gain.1) | copy-start | bytes 24580
  2.9 56.0 %copy-start.2 = (f32[1,4,2304]{2,1,0:T(4,128)S(1)}, f32[1,4,2304]{2,1,0:T(4,128)}, u32[]{:S(2)}) copy-start(f32[1,4,2304]{2,1,0:T(4,128)} %param.14) | copy-start | bytes 110596
  2.9 56.0 %copy-start.3 = (f32[1,2304]{1,0:T(1,128)S(1)}, f32[1,2304]{1,0:T(1,128)}, u32[]{:S(2)}) copy-start(f32[1,2304]{1,0:T(1,128)} %cb.1) | copy-start | bytes 27652
  2.9 56.0 %copy-start.5 = (f32[1,2048]{1,0:T(1,128)S(1)}, f32[1,2048]{1,0:T(1,128)}, u32[]{:S(2)}) copy-start(f32[1,2048]{1,0:T(1,128)} %gg.1) | copy-start | bytes 24580
  2.9 56.0 %copy-start.6 = (f32[1,256]{1,0:T(1,128)S(1)}, f32[1,256]{1,0:T(1,128)}, u32[]{:S(2)}) copy-start(f32[1,256]{1,0:T(1,128)} %lb.1) | copy-start | bytes 3076
  2.9 56.0 %copy-start.7 = (f32[1,32]{1,0:T(1,128)S(1)}, f32[1,32]{1,0:T(1,128)}, u32[]{:S(2)}) copy-start(f32[1,32]{1,0:T(1,128)} %dtb.1) | copy-start | bytes 388
  2.9 55.9 %copy-start.8 = (f32[1,32]{1,0:T(1,128)S(1)}, f32[1,32]{1,0:T(1,128)}, u32[]{:S(2)}) copy-start(f32[1,32]{1,0:T(1,128)} %rate.1) | copy-start | bytes 388
  2.9 55.9 %copy-start.9 = (f32[1,32]{1,0:T(1,128)S(1)}, f32[1,32]{1,0:T(1,128)}, u32[]{:S(2)}) copy-start(f32[1,32]{1,0:T(1,128)} %skip.1) | copy-start | bytes 388
  57.3 1.6 %copy-start = (bf16[1024,1408]{1,0:T(8,128)(2,1)}, bf16[1024,1408]{1,0:T(8,128)(2,1)S(1)}, u32[]{:S(2)}) copy-start(bf16[1024,1408]{1,0:T(8,128)(2,1)S(1)} %gather_project.1.p) | copy-start | bytes 8650756

commit v2 on v0

v2 whole, which is shorter than its diff:
```python
import functools
import jax
import jax.numpy as jnp
from jax import lax
from jax.experimental import pallas as pl
from jax.experimental.pallas import tpu as pltpu
from jax.sharding import PartitionSpec as P

EPS = 1e-05
MESH = pl.DeviceIdType.MESH
NX, NZ, NY = 4, 8, 4
GROUPS = NX * NZ
CA, CB = 512, 896
NP = CA + CB
ROWS = 256
F32, BF16 = jnp.float32, jnp.bfloat16


def seq_of(x, z, y):
    return (lax.rem(x + 4 * NX, NX) * NZ + lax.rem(z + 4 * NZ, NZ)) * NY + lax.rem(y + 4 * NY, NY)


def plan():
    msgs = {}
    ua, ub, un = 64 * CA * 2, 64 * CB * 2, 128 * 2048 * 2
    for d, links in ((1, {"y+": 1}), (3, {"y-": 1}), (2, {"y+": 1, "y-": 1})):
        msgs[("w", d)] = ("w", None, (0, 0, d), None, 16 * NP * 2, links)
    msgs[("P", 0)] = ("h0", 0, (0, 0, 1), None, un, {"y+": 1})
    msgs[("M", 1)] = ("h1", 0, (0, 0, -1), None, un, {"y-": 1})
    msgs[("P", 1)] = ("h1", 0, (0, 0, 1), None, un, {"y+": 1})
    msgs[("M", 0)] = ("h0", 0, (0, 0, -1), None, un, {"y-": 1})
    msgs[("P", 2)] = ("h0", -1, (0, 0, 1), ("P", 0), un, {"y+": 1})
    msgs[("M", 2)] = ("h1", 1, (0, 0, -1), ("M", 1), un, {"y-": 1})
    own = "own"
    for d, links in ((1, {"x+": 1}), (3, {"x-": 1}), (2, {"x+": 2})):
        msgs[("A1", d)] = ("a", (0, 0), (d, 0, 0), own, ua, links)
    for k in range(1, 5):
        if k < 5:
            dep = own if k == 1 else ("B1+", k - 1)
            msgs[("B1+", k)] = ("b", (0, -(k - 1)), (0, 1, 0), dep, ub, {"z+": 1})
        if k < 4:
            dep = own if k == 1 else ("B1-", k - 1)
            msgs[("B1-", k)] = ("b", (0, k - 1), (0, -1, 0), dep, ub, {"z-": 1})
    for k in range(1, 5):
        for d in range(4):
            up, down = (4, 3) if d < 2 else (3, 4)
            if k <= up:
                dep = (own if d == 0 else ("A1", d)) if k == 1 else ("A2+", d, k - 1)
                msgs[("A2+", d, k)] = ("a", (-d, -(k - 1)), (0, 1, 0), dep, ua, {"z+": 1})
            if k <= down:
                dep = (own if d == 0 else ("A1", d)) if k == 1 else ("A2-", d, k - 1)
                msgs[("A2-", d, k)] = ("a", (-d, k - 1), (0, -1, 0), dep, ua, {"z-": 1})
    offs = [0, -1, 1, -2, 2, -3, 3, -4]
    for n, o in enumerate(offs):
        dep = own if o == 0 else (("B1+", -o) if o < 0 else ("B1-", o))
        msgs[("B2+", o)] = ("b", (0, o), (1, 0, 0), dep, ub, {"x+": 1})
        msgs[("B2-", o)] = ("b", (0, o), (-1, 0, 0), dep, ub, {"x-": 1})
        if n in (1, 3, 5):
            msgs[("B2+2", o)] = ("b", (-1, o), (1, 0, 0), ("B2+", o), ub, {"x+": 1})
        else:
            msgs[("B2-2", o)] = ("b", (1, o), (-1, 0, 0), ("B2-", o), ub, {"x-": 1})
    return msgs


def schedule(msgs, rate=46.6e3, latency=1.9):
    free, arrive, order = {}, {}, []
    started = set()
    events = []

    def start(name, now):
        part, chunk, to, dep, size, links = msgs[name]
        begin = max([now] + [free.get(l, 0.0) for l in links])
        end = begin
        for l, n in links.items():
            free[l] = begin + size * n / rate
            end = max(end, free[l])
        arrive[name] = end + latency
        events.append((end + latency, len(started), name))
        started.add(name)

    for name, m in msgs.items():
        if m[3] is None:
            start(name, 0.0)
    got = set()
    while events:
        events.sort()
        now, _, name = events.pop(0)
        order.append(name)
        got.add(name)
        if all(("w", d) in got for d in (1, 2, 3)) and "own" not in got:
            got.add("own")
            order.append("own")
            for other, m in msgs.items():
                if m[3] == "own":
                    start(other, now)
        for other, m in msgs.items():
            if m[3] == name:
                start(other, now)
    return order, arrive


HI = lax.Precision.HIGHEST
MID = CA + 768
LEVELS_OUT = 5
TABLE = (0, 16, 24, 28, 30)


def spread(row, lanes):
    k = lax.broadcasted_iota(jnp.int32, (128, lanes), 0)
    c = lax.broadcasted_iota(jnp.int32, (128, lanes), 1)
    return jnp.dot(row, (k == 64 + 8 * lax.shift_right_logical(c, 6)).astype(F32), precision=HI, preferred_element_type=F32)


def halves_of(a, lane_low, lane_high, first):
    return jnp.where(first, a[:, lane_low : lane_low + 1], a[:, lane_high : lane_high + 1])


def softplus(v):
    return jnp.maximum(v, 0.0) + jnp.log1p(jnp.exp(-jnp.abs(v)))


def layer_kernel(acts_in, proj_in, wout_in, gain_in, cw_in, cb_in, dtb_in, rate_in, skip_in, lb_in, gg_in, out,
                 wa, wb, ablk, u, p, proj, small,
                 gain, cw, cb, dtb, rate, skip, lb, gg,
                 ext, xf, bcs, td, cu, yacc, near_st, eb, ee, snd1, slog, rcv1, rlog, table, rcv2, tail,
                 qs, qr, wout, acc, os, oin,
                 local_sems, send_sems, recv_sems, in_sems,
                 ssem, rsem, lsend, lrecv, tsem, qsend, qrecv, osend, orecv, dsem):
    i = lax.axis_index("seq")
    y = lax.rem(i, NY)
    g = lax.div(i, NY)
    z = lax.rem(g, NZ)
    x = lax.div(g, NZ)
    s = lax.axis_index("section")

    def there(dx, dz, dy):
        return {"seq": seq_of(x + dx, z + dz, y + dy)}

    def group(n):
        return {"seq": n * NY + y}

    def beside(n):
        return {"seq": g * NY + lax.rem(y + n, NY)}

    def wrap(n):
        return lax.rem(n, GROUPS)

    def remote(src, dst, send, recv, to):
        return pltpu.make_async_remote_copy(
            src_ref=src, dst_ref=dst, send_sem=send, recv_sem=recv, device_id=to, device_id_type=MESH)

    with jax.named_scope("enter"):
        barrier = pltpu.get_barrier_semaphore()

        def greet(d, _):
            pl.semaphore_signal(barrier, inc=1, device_id=group(wrap(g + d)), device_id_type=MESH)
            return 0

        lax.fori_loop(1, GROUPS, greet, 0)
        for d in (1, 2, 3):
            pl.semaphore_signal(barrier, inc=1, device_id=beside(d), device_id_type=MESH)
        pl.semaphore_signal(barrier, inc=1, device_id={"section": 1 - s}, device_id_type=MESH)
        pairs = ((proj_in, proj), (acts_in, ablk.at[y]), (gain_in, gain), (cw_in, cw), (cb_in, cb), (dtb_in, dtb),
                 (rate_in, rate), (skip_in, skip), (lb_in, lb), (gg_in, gg), (wout_in, wout))
        loads = [pltpu.make_async_copy(a, b, in_sems.at[n]) for n, (a, b) in enumerate(pairs)]
        for copy in loads[:-1]:
            copy.start()

        loads[0].wait()
        rows_k = lax.broadcasted_iota(jnp.int32, (288, 128), 0)
        lane_k = lax.broadcasted_iota(jnp.int32, (288, 128), 1)
        packed = proj[:, 4352:]
        for n in range(NY):
            from_lr = (lane_k < 64) & (rows_k == 32 + 64 * n + lane_k)
            from_dr = (lane_k >= 64) & (rows_k == 8 * n + lax.shift_right_logical(lane_k - 64, 3))
            hit = (from_lr | from_dr).astype(BF16)
            small[n] = jnp.dot(packed, hit, preferred_element_type=F32).astype(BF16)

        msgs = plan()
        number = {name: n for n, name in enumerate(msgs)}
        order, _ = schedule(msgs)

        def block(rel):
            return lax.rem(y + rel + 2 * NY, NY)

        def rows_of(cx, cz):
            return pl.ds(pl.multiple_of(seq_of(x + cx, z + cz, 0) * 16, 64), 64)

        def pieces(slot, rows):
            cols = pl.multiple_of(slot * 512, 512)
            return [(proj.at[:, pl.ds(cols, 512)], wa.at[rows]),
                    (proj.at[:, pl.ds(2048, 256)], wb.at[rows, pl.ds(0, 256)]),
                    (proj.at[:, pl.ds(pl.multiple_of(2304 + cols, 256), 512)], wb.at[rows, pl.ds(256, 512)]),
                    (small.at[slot], wb.at[rows, pl.ds(768, 128)])]

        mine = pl.ds(pl.multiple_of(i * 16, 16), 16)
        local = [pltpu.make_async_copy(a, b, local_sems.at[n]) for n, (a, b) in enumerate(pieces(y, mine))]
        for copy in local:
            copy.start()
        loads[1].wait()
        pl.semaphore_wait(barrier, GROUPS - 1 + 3 + 1)

    def copies(name, arriving):
        part, chunk, to, dep, _, _ = msgs[name]
        n = number[name]
        back = to if arriving else (0, 0, 0)
        if part == "w":
            d = to[2]
            rows = pl.ds(pl.multiple_of(seq_of(x, z, y - d) * 16, 16), 16) if arriving else mine
            slot = lax.rem(y + d, NY)
            return [remote(a, b, send_sems.at[n if e == 0 else len(msgs) + 3 * n + e], recv_sems.at[n if e == 0 else len(msgs) + 3 * n + e], there(*to))
                    for e, (a, b) in enumerate(pieces(slot, rows))]
        if part in ("h0", "h1"):
            ref = ablk.at[block(chunk - back[2]), pl.ds(128 * int(part[1]), 128)]
        else:
            ref = (wa if part == "a" else wb).at[rows_of(chunk[0] - back[0], chunk[1] - back[1])]
        return [remote(ref, ref, send_sems.at[n], recv_sems.at[n], there(*to))]

    def start(name):
        for copy in copies(name, False):
            copy.start()

    def normed(rel, half):
        def step(n, _):
            at = pl.multiple_of(half * 128 + n * 64, 64)
            b = block(rel)
            h = ablk[b, pl.ds(at, 64), :].astype(F32)
            r = lax.rsqrt(jnp.mean(h * h, axis=1, keepdims=True) + EPS)
            u[pl.ds(pl.multiple_of(b * ROWS + at, 64), 64), :] = (h * r * gain[...]).astype(BF16)
            return 0

        lax.fori_loop(0, 2, step, 0)

    with jax.named_scope("gather"):
        for name, m in msgs.items():
            if m[3] is None:
                start(name)
        for copy in loads[2:-1]:
            copy.wait()
        loads[-1].start()
        normed(0, 0)
        normed(0, 1)
        halves = {("P", 0): (-1, 0), ("P", 1): (-1, 1), ("M", 1): (1, 1), ("M", 0): (1, 0), ("P", 2): (-2, 0), ("M", 2): (2, 1)}
        for name in order:
            if name == "own":
                for copy in local:
                    copy.wait()
            else:
                for copy in copies(name, True):
                    copy.wait_recv()
            for other, m in msgs.items():
                if m[3] == name:
                    start(other)
            if name in halves:
                normed(*halves[name])

    def product(n, _):
        rows = pl.ds(pl.multiple_of(n * 512, 512), 512)
        p[rows, :CA] = jnp.dot(u[rows, :], wa[...], preferred_element_type=F32).astype(BF16)
        p[rows, CA:] = jnp.dot(u[rows, :], wb[...], preferred_element_type=F32).astype(BF16)
        return 0

    with jax.named_scope("project"):
        lax.fori_loop(0, 2, product, 0)

    with jax.named_scope("rows"):
        def picked(v, hit):
            rows = jnp.broadcast_to(v[...], (8, v.shape[1]))
            return jnp.dot(rows, hit.astype(F32), precision=HI, preferred_element_type=F32)[:1]

        def two(rows, lanes):
            return (lax.broadcasted_iota(jnp.int32, (rows, lanes), 0), lax.broadcasted_iota(jnp.int32, (rows, lanes), 1))

        k, c = two(32, 128)
        of_head = (c >= 64) & (k == 8 * y + lax.shift_right_logical(c - 64, 3))
        k2, c2 = two(256, 128)
        bias = picked(dtb, of_head) + picked(lb, (c2 < 64) & (k2 == 64 * y + c2))
        rates = picked(rate, of_head)
        k3, c3 = two(32, 512)
        skips = picked(skip, k3 == 8 * y + lax.shift_right_logical(c3, 6))

        low_tri = (lax.broadcasted_iota(jnp.int32, (ROWS, ROWS), 1) <= lax.broadcasted_iota(jnp.int32, (ROWS, ROWS), 0)).astype(BF16)
        for b in range(4):
            rows = slice(b * ROWS, (b + 1) * ROWS)
            t = softplus(p[rows, MID:].astype(F32) + bias)
            td[rows, :] = t
            left = -t * rates
            total = jnp.zeros((ROWS, 128), F32)
            for _ in range(3):
                piece = left.astype(BF16)
                total = total + jnp.dot(low_tri, piece, preferred_element_type=F32)
                left = left - piece.astype(F32)
            cu[rows, :] = total
            eb[b : b + 1, :] = total[ROWS - 1 :, :]
        eb[4:, :] = jnp.zeros((4, 128), F32)
        ends = eb[...]
        ee[...] = jnp.exp(spread(ends, 512))
        slog[...] = jnp.broadcast_to(jnp.sum(ends, axis=0, keepdims=True), (8, 128))

    with jax.named_scope("conv"):
        back = remote(p.at[pl.ds(1008, 16), pl.ds(0, 768)], tail, tsem.at[0], tsem.at[1], group(wrap(g + 1)))
        back.start()

        for n in range(4):
            ext[8 + n * ROWS : 8 + (n + 1) * ROWS, :] = p[n * ROWS : (n + 1) * ROWS, :768].astype(F32)
        own = pl.ds(pl.multiple_of(y * 512, 512), 512)
        tx = [cw[k : k + 1, own] for k in range(4)]
        tb = [cw[k : k + 1, 2048:] for k in range(4)]
        bx, bb = cb[:, own], cb[:, 2048:]

        def convolved(n):
            at = n * 128
            v = bx
            for k in range(4):
                v = v + tx[k] * ext[at + 5 + k : at + 133 + k, :512]
            xf[at : at + 128, :] = jax.nn.silu(v)
            v = bb
            for k in range(4):
                v = v + tb[k] * ext[at + 5 + k : at + 133 + k, 512:]
            bcs[at : at + 128, :] = jax.nn.silu(v).astype(BF16)

        for n in range(1, 8):
            convolved(n)
        back.wait_recv()
        before = tail[...].astype(F32)
        ext[0:8, :] = jnp.where(g > 0, before[8:, :], 0.0)
        convolved(0)

    with jax.named_scope("states"):
        first = lax.broadcasted_iota(jnp.int32, (1, 128), 1) < 64

        def state(b):
            rows = slice(b * ROWS, (b + 1) * ROWS)
            tl = jnp.exp(ends[b : b + 1, :] - cu[rows, :]) * td[rows, :]
            parts = []
            for h in range(4):
                parts.append((xf[rows, 128 * h : 128 * h + 128] * halves_of(tl, 64 + 16 * h, 72 + 16 * h, first)).astype(BF16))
            xt = jnp.concatenate(parts, axis=1)
            return lax.dot_general(bcs[rows, :128], xt, (((0,), (0,)), ((), ())), preferred_element_type=F32)

        st = state(0)
        near_st[0] = st.astype(BF16)
        st = ee[1:2, :] * st + state(1)
        near_st[1] = st.astype(BF16)
        other = state(2)
        near_st[2] = other.astype(BF16)
        st = ee[2:3, :] * ee[3:4, :] * st + ee[3:4, :] * other + state(3)
        st = st.astype(BF16)
        for n in range(GROUPS):
            ct, nt = n // 8, n % 8
            snd1[n] = st[16 * nt : 16 * nt + 16, 128 * ct : 128 * ct + 128]

        def first_send(d, _):
            to = wrap(g + d)
            remote(snd1.at[to], rcv1.at[g], ssem.at[0], rsem.at[0], group(to)).start()
            remote(slog, rlog.at[g], ssem.at[1], rsem.at[1], group(to)).start()
            return 0

        lax.fori_loop(1, GROUPS, first_send, 0)
        rcv1[g] = snd1[g]
        rlog[g] = slog[...]

    with jax.named_scope("inside"):
        def inside(b, _):
            base = pl.multiple_of(b * ROWS, ROWS)
            every = pl.ds(base, ROWS)
            cum_t = jnp.transpose(cu[every, :])
            dt_t = jnp.transpose(td[every, :])
            for r in range(2):
                rows = pl.ds(pl.multiple_of(base + 128 * r, 128), 128)
                wide = 128 * (r + 1)
                seen = pl.ds(base, wide)
                scores = lax.dot_general(bcs[rows, 128:], bcs[seen, :128], (((1,), (1,)), ((), ())), preferred_element_type=F32)
                ti, si = two(128, wide)
                causal = si <= ti + 128 * r
                cum, lam = cu[rows, :], td[rows, :]
                for h in range(4):
                    xp = xf[seen, 128 * h : 128 * h + 128].astype(BF16)
                    got = []
                    for e in (2 * h, 2 * h + 1):
                        lane = 64 + 8 * e
                        differ = jnp.where(causal, cum[:, lane : lane + 1] - cum_t[lane : lane + 1, :wide], -1e30)
                        w = scores * jnp.exp(differ) * dt_t[lane : lane + 1, :wide]
                        got.append(jnp.dot(w.astype(BF16), xp, preferred_element_type=F32))
                    val = jnp.where(first, got[0], got[1]) * halves_of(lam, 16 * h, 16 * h + 8, first)
                    cols = slice(128 * h, 128 * h + 128)
                    yacc[rows, cols] = val + skips[:, cols] * xf[rows, cols]
            return 0

        lax.fori_loop(0, 4, inside, 0)

    with jax.named_scope("wait1"):
        remote(rcv1.at[pl.ds(0, GROUPS - 1)], rcv1.at[pl.ds(0, GROUPS - 1)], ssem.at[0], rsem.at[0], group(g)).wait_recv()
        remote(rlog.at[pl.ds(0, GROUPS - 1)], rlog.at[pl.ds(0, GROUPS - 1)], ssem.at[1], rsem.at[1], group(g)).wait_recv()
    with jax.named_scope("merge"):
        logs = rlog[:, 0, :]
        wide_logs = spread(logs, 512)
        ct = lax.div(g, 8)
        head_logs = jnp.zeros((GROUPS, 128), F32)
        for n in range(4):
            head_logs = jnp.where(ct == n, wide_logs[:, 128 * n : 128 * n + 128], head_logs)
        level = [rcv1[n].astype(F32) for n in range(GROUPS)]
        ends_of = [head_logs[n : n + 1, :] for n in range(GROUPS)]
        for l in range(LEVELS_OUT):
            for n in range(0, len(level), 2):
                table[TABLE[l] + n // 2] = level[n].astype(BF16)
            level = [jnp.exp(ends_of[n + 1]) * level[n] + level[n + 1] for n in range(0, len(level), 2)]
            ends_of = [ends_of[n] + ends_of[n + 1] for n in range(0, len(ends_of), 2)]

        def second_send(d, _):
            to = wrap(g + d)
            for l in range(LEVELS_OUT):
                up = lax.div(to, 2**l)

                @pl.when(lax.rem(up, 2) == 1)
                def _():
                    remote(table.at[TABLE[l] + lax.div(up, 2)], rcv2.at[l, g], lsend.at[l], lrecv.at[l], group(to)).start()

            return 0

        lax.fori_loop(1, GROUPS, second_send, 0)
    with jax.named_scope("near"):
        bits = [lax.rem(lax.div(g, 2**l), 2) for l in range(LEVELS_OUT)]

        lane8 = lax.broadcasted_iota(jnp.int32, (1, 128), 1) & 7

        def read(b, rows, bucket, scale, lev):
            r = jnp.dot(bcs[rows, 128:], bucket, preferred_element_type=F32)
            for h in range(4):
                cols = slice(128 * h, 128 * h + 128)
                yacc[rows, cols] += r[:, cols] * halves_of(scale, 16 * h + lev, 16 * h + 8 + lev, first)

        def scales(rows, add):
            return pltpu.roll(jnp.exp(cu[rows, :] + add), 64, 1) * td[rows, :]

        zero = jnp.zeros((1, 128), F32)
        at_block = [pl.ds(b * ROWS, ROWS) for b in range(4)]
        read(1, at_block[1], near_st[0], scales(at_block[1], zero), 1)
        read(2, at_block[2], near_st[1], scales(at_block[2], zero), 2)
        sc = scales(at_block[3], jnp.where(lane8 == 2, ends[2:3, :], 0.0))
        read(3, at_block[3], near_st[2], sc, 1)
        read(3, at_block[3], near_st[1], sc, 2)

        row_of = lax.broadcasted_iota(jnp.int32, (GROUPS, 1), 0)
        outer = zero
        for l in range(LEVELS_OUT):
            start = lax.div(g, 2**l) * 2**l
            summed = jnp.sum(jnp.where((row_of >= start) & (row_of < g), logs, 0.0), axis=0, keepdims=True)
            outer = jnp.where(lane8 == l + 3, summed, outer)
        run = zero
        for b in range(4):
            eb[4 + b : 5 + b, :] = run + outer
            run = run + ends[b : b + 1, :]

    with jax.named_scope("wait2"):
        for l in range(LEVELS_OUT):
            @pl.when(bits[l] == 1)
            def _():
                remote(rcv2.at[l, pl.ds(0, GROUPS - 1)], rcv2.at[l, pl.ds(0, GROUPS - 1)], lsend.at[l], lrecv.at[l], group(g)).wait_recv()
                rcv2[l, g] = table[TABLE[l] + lax.div(g, 2 ** (l + 1))]

            @pl.when(bits[l] == 0)
            def _():
                rcv2[l] = jnp.zeros((GROUPS, 16, 128), BF16)

    with jax.named_scope("finish"):
        def finish(n, _):
            b = lax.rem(y + n, NY)
            base = pl.multiple_of(b * ROWS, ROWS)
            for half in range(2):
                rows = pl.ds(pl.multiple_of(base + 128 * half, 128), 128)
                scale = scales(rows, eb[pl.ds(4 + b, 1), :])
                c = bcs[rows, 128:]
                for h in range(0, 4, 2):
                    vals = [yacc[rows, 128 * (h + e) : 128 * (h + e) + 128] for e in range(2)]
                    for l in range(LEVELS_OUT):
                        pair = [rcv2[l, 8 * (h + e) : 8 * (h + e) + 8].reshape(128, 128) for e in range(2)]
                        r = jnp.dot(c, jnp.concatenate(pair, axis=1), preferred_element_type=F32)
                        for e in range(2):
                            lane = 16 * (h + e) + l + 3
                            vals[e] = vals[e] + r[:, 128 * e : 128 * e + 128] * halves_of(scale, lane, lane + 8, first)
                    for e in range(2):
                        cols = slice(128 * (h + e), 128 * (h + e) + 128)
                        zg = p[rows, 768 + 128 * (h + e) : 896 + 128 * (h + e)].astype(F32)
                        qs[b, 128 * half : 128 * half + 128, cols] = (vals[e] * jax.nn.silu(zg)).astype(BF16)

            @pl.when(n < 4)
            def _():
                remote(qs.at[b], qr.at[y], qsend.at[n], qrecv.at[n], beside(n)).start()

            return 0

        lax.fori_loop(1, 5, finish, 0)
    with jax.named_scope("out"):
        qr[y] = qs[y]
        loads[-1].wait()

        squares = jnp.zeros((ROWS, 1), F32)
        for at, n in enumerate((0, 1, 3, 2)):
            src = lax.rem(y + NY - n, NY)
            if n:
                remote(qs.at[0], qr.at[src], qsend.at[n], qrecv.at[n], beside(n)).wait_recv()
            v = qr[src].astype(F32)
            squares = squares + jnp.sum(v * v, axis=1, keepdims=True)
            lanes = pl.ds(pl.multiple_of(src * 512, 512), 512)
            v = (v * gg[:, lanes]).astype(BF16)
            for t in range(4):
                cols = slice(512 * t, 512 * t + 512)
                part = jnp.dot(v, wout[lanes, cols], preferred_element_type=F32)
                acc[:, cols] = part if at == 0 else acc[:, cols] + part
    with jax.named_scope("swap"):
        r = lax.rsqrt(squares * (1.0 / 2048.0) + EPS)
        sends = []
        for t in range(4):
            cols = slice(512 * t, 512 * t + 512)
            os[t] = (ablk[y, :, cols].astype(F32) + r * acc[:, cols]).astype(BF16)
            sends.append(remote(os.at[t], oin.at[t], osend.at[t], orecv.at[t], {"section": 1 - s}))
            sends[-1].start()
        stores = []
        for t in range(4):
            sends[t].wait_recv()
            stores.append(pltpu.make_async_copy(oin.at[t], out.at[:, pl.ds(512 * t, 512)], dsem.at[t]))
            stores[-1].start()
    with jax.named_scope("drain"):
        for name in msgs:
            for copy in copies(name, False):
                copy.wait_send()
        back.wait_send()
        remote(rcv1.at[pl.ds(0, GROUPS - 1)], rcv1.at[pl.ds(0, GROUPS - 1)], ssem.at[0], rsem.at[0], group(g)).wait_send()
        remote(rlog.at[pl.ds(0, GROUPS - 1)], rlog.at[pl.ds(0, GROUPS - 1)], ssem.at[1], rsem.at[1], group(g)).wait_send()
        for l in range(LEVELS_OUT):
            for bit in range(2):
                @pl.when(bits[l] == bit)
                def _():
                    some = rcv2.at[l, pl.ds(0, 16 - bit)]
                    remote(some, some, lsend.at[l], lrecv.at[l], group(g)).wait_send()
        for n in (1, 2, 3):
            remote(qs.at[0], qr.at[y], qsend.at[n], qrecv.at[n], beside(n)).wait_send()
        for copy in sends:
            copy.wait_send()
        for copy in stores:
            copy.wait()


def layer(acts, proj, wout, *params):
    anywhere = pl.BlockSpec(memory_space=pl.ANY)
    n = NY * ROWS
    count = 4 * len(plan())
    dma = pltpu.SemaphoreType.DMA
    return pl.pallas_call(
        layer_kernel,
        out_shape=jax.ShapeDtypeStruct((ROWS, 2048), BF16),
        in_specs=[anywhere] * (3 + len(params)),
        out_specs=anywhere,
        scratch_shapes=[
            pltpu.VMEM((2048, CA), BF16),
            pltpu.VMEM((2048, CB), BF16),
            pltpu.VMEM((NY, ROWS, 2048), BF16),
            pltpu.VMEM((n, 2048), BF16),
            pltpu.VMEM((n, NP), BF16),
            pltpu.VMEM(proj.shape, BF16),
            pltpu.VMEM((NY, 16, 128), BF16),
            *[pltpu.VMEM(a.shape, a.dtype) for a in params],
            pltpu.VMEM((n + 8, 768), F32),
            pltpu.VMEM((n, 512), F32),
            pltpu.VMEM((n, 256), BF16),
            pltpu.VMEM((n, 128), F32),
            pltpu.VMEM((n, 128), F32),
            pltpu.VMEM((n, 512), F32),
            pltpu.VMEM((3, 128, 512), BF16),
            pltpu.VMEM((8, 128), F32),
            pltpu.VMEM((8, 512), F32),
            pltpu.VMEM((GROUPS, 16, 128), BF16),
            pltpu.VMEM((8, 128), F32),
            pltpu.VMEM((GROUPS, 16, 128), BF16),
            pltpu.VMEM((GROUPS, 8, 128), F32),
            pltpu.VMEM((31, 16, 128), BF16),
            pltpu.VMEM((LEVELS_OUT, GROUPS, 16, 128), BF16),
            pltpu.VMEM((16, 768), BF16),
            pltpu.VMEM((NY, ROWS, 512), BF16),
            pltpu.VMEM((NY, ROWS, 512), BF16),
            pltpu.VMEM((2048, 2048), BF16),
            pltpu.VMEM((ROWS, 2048), F32),
            pltpu.VMEM((4, ROWS, 512), BF16),
            pltpu.VMEM((4, ROWS, 512), BF16),
            dma((4,)), dma((count,)), dma((count,)), dma((11,)),
            dma((2,)), dma((2,)), dma((5,)), dma((5,)), dma((2,)), dma((4,)), dma((4,)), dma((4,)), dma((4,)), dma((4,)),
        ],
        compiler_params=pltpu.CompilerParams(
            collective_id=0, has_side_effects=True, vmem_limit_bytes=62 * 1024 * 1024),
        name="layer",
    )(acts, proj, wout, *params)


def per_device(acts, in_proj, out_proj, conv_weight, conv_bias, dt_bias, decay_rate, skip_gain, level_bias, norm_gain, gate_gain):
    o = layer(acts[0], in_proj[0], out_proj[0], norm_gain, conv_weight[0], conv_bias, dt_bias, decay_rate, skip_gain, level_bias, gate_gain)
    return o[None]


def solution(mesh):
    two = P("section", None)
    three = P("section", None, None)
    return jax.shard_map(
        per_device,
        mesh=mesh,
        in_specs=(P("section", "seq", None), P("section", "seq", None), three, three, two, two, two, two, two, two, two),
        out_specs=P("section", "seq", None),
        check_vma=False,
    )
```

time: 253 us -> 109 us (0.43); the launches traced: 250 us -> 109 us
  local copies, waits for them, and re-layouts: 73.9 us -> 2.3 us
  Pallas kernels: 54.1 us -> 107 us
  starting transfers between devices: 39.8 us -> 0 us
  waiting for transfers between devices: 29.9 us -> 0 us
  matrix products: 26.2 us -> 0 us
  other arithmetic: 24 us -> 0 us
    pallas_call x1, Pallas kernels: 54.1 us -> 107 us  [layer(): pl.pallas_call(layer_kernel, out_shape=jax.ShapeDtypeStruct((ROWS, 2048),...]
    ppermute x14 -> x0, starting transfers between devices: 39.8 us -> none  [the longest x1 17.3 us: per_device(): return lax.ppermute(o, 'section', [(0, 1), (1, 0)])[None]]
    ppermute x14 -> x0, waiting for transfers between devices: 29.9 us -> none  [the longest x9 21.6 us: swapped(): return lax.ppermute(block, 'seq', route)]
    mul x33 -> x0, local copies, waits for them, and re-layouts: 22 us -> none  [the longest x24 18.5 us: read(): return r * (lam[n, :, :, level] * jnp.exp(cum[n] + before))[..., None]]
    dot_general x13 -> x0, matrix products: 18.1 us -> none  [the longest x1 5.73 us: per_device(): jnp.dot(n, out_proj[0], preferred_element_type=F32)]
    slice x26 -> x0, local copies, waits for them, and re-layouts: 17.9 us -> none  [the longest x3 6.12 us: per_device(): x[n] * (jnp.exp(end[n] - cum[n]) * dt[n])[..., None]]
    unnamed x168 -> x1, local copies, waits for them, and re-layouts: 13.4 us -> 2.3 us
    reshape x8 -> x0, local copies, waits for them, and re-layouts: 9.51 us -> none  [the longest x2 7.8 us: per_device(): jnp.stack(yb).reshape(1024, 8, 64)]
  transfers between devices with their start and end apart: 14 -> 0, of which waited for: 11 -> 0; matrix products, arithmetic and copies ran while one was open for 27% -> 0% of each run, Pallas kernels for 0% -> 0%
where the time goes in v2:
time: 109 us
  Pallas kernels  107 us (98%)
  local copies, waits for them, and re-layouts  2.3 us (2%)
    pallas_call x1, Pallas kernels, layer(): pl.pallas_call(layer_kernel, out_shape=jax.ShapeDtypeStruct((ROWS, 2048),...  107 us
    unnamed x1, local copies, waits for them, and re-layouts  2.3 us

profile of v2, /device:TPU:3, one launch (start us, length us, event | category | flops | bytes accessed | tf_op | source)
XLA Modules:
  0.0 109.0 jit_solution(17503221061311372640)
XLA Ops:
  0.0 106.7 %layer.1 = bf16[256,2048]{1,0:T(8,128)(2,1)} custom-call(bf16[256,2048]{1,0:T(8,128)(2,1)} %bitcast.7, bf16[16,4640]{1,0:T(8,128)(2,1)} %bitcast.8, bf16[2048,2048]{1,0:T(8,128)(2,1)} %bitcast.5, f32[1,2048]{1,0:T(1,128)} %gain_in.1, f32[4,2304]{1,0:T(4,128)} %bitcast.9, f32[1,2304]{1,0:T(1,128)} %cb_in.1, f32[1,32]{1,0:T(1,128)} %dtb_in.1, ...), custom_call_target="tpu_custom_call" | custom-call | tf_op jit(solution)/shard_map/layer/pallas_call | solution.py:550
  106.7 2.3 %copy.13 = bf16[1,256,2048]{2,1,0:T(8,128)(2,1)} copy(bf16[1,256,2048]{2,1,0:T(8,128)(2,1)} %bitcast.6) | data formatting | bytes 2097152

commit v3 on v2

--- a/solution.py
+++ b/solution.py
@@ -120,12 +120,12 @@
 
 
 def layer_kernel(acts_in, proj_in, wout_in, gain_in, cw_in, cb_in, dtb_in, rate_in, skip_in, lb_in, gg_in, out,
-                 wa, wb, ablk, u, p, proj, small,
+                 wa, wb, ablk, u, pacc, p, proj, small, ones,
                  gain, cw, cb, dtb, rate, skip, lb, gg,
                  ext, xf, bcs, td, cu, yacc, near_st, eb, ee, snd1, slog, rcv1, rlog, table, rcv2, tail,
-                 qs, qr, wout, acc, os, oin,
+                 qs, qr, wout, acc, os,
                  local_sems, send_sems, recv_sems, in_sems,
-                 ssem, rsem, lsend, lrecv, tsem, qsend, qrecv, osend, orecv, dsem):
+                 ssem, rsem, lsend, lrecv, tsem, qsend, qrecv, osend, orecv):
     i = lax.axis_index("seq")
     y = lax.rem(i, NY)
     g = lax.div(i, NY)
@@ -240,7 +240,56 @@
         loads[-1].start()
         normed(0, 0)
         normed(0, 1)
+        def picked(v, hit):
+            rows = jnp.broadcast_to(v[...], (8, v.shape[1]))
+            return jnp.dot(rows, hit.astype(F32), precision=HI, preferred_element_type=F32)[:1]
+
+        def two(rows, lanes):
+            return (lax.broadcasted_iota(jnp.int32, (rows, lanes), 0), lax.broadcasted_iota(jnp.int32, (rows, lanes), 1))
+
+        k, c = two(32, 128)
+        of_head = (c >= 64) & (k == 8 * y + lax.shift_right_logical(c - 64, 3))
+        k2, c2 = two(256, 128)
+        bias = picked(dtb, of_head) + picked(lb, (c2 < 64) & (k2 == 64 * y + c2))
+        rates = picked(rate, of_head)
+        k3, c3 = two(32, 512)
+        skips = picked(skip, k3 == 8 * y + lax.shift_right_logical(c3, 6))
+
+        low_tri = (lax.broadcasted_iota(jnp.int32, (ROWS, ROWS), 1) <= lax.broadcasted_iota(jnp.int32, (ROWS, ROWS), 0)).astype(BF16)
+        lane_in, col_in = two(256, 512)
+        for lev in range(9):
+            lane = lev + 8 * lax.shift_right_logical(col_in, 6) + (64 - 8 if lev == 8 else 0)
+            ones[lev] = ((lane_in & 127) == lane).astype(BF16)
+
+        def widened(v, lev):
+            high = v.astype(BF16)
+            low = (v - high.astype(F32)).astype(BF16)
+            return jnp.concatenate([high, low], axis=1), lev
+
+        def wide(pair, cols=slice(0, 512)):
+            return jnp.dot(pair[0], ones[pair[1], :, cols], preferred_element_type=F32)
+
         halves = {("P", 0): (-1, 0), ("P", 1): (-1, 1), ("M", 1): (1, 1), ("M", 0): (1, 0), ("P", 2): (-2, 0), ("M", 2): (2, 1)}
+        missing = {d: set() for d in range(NX)}
+        for name, m in msgs.items():
+            if m[0] in ("a", "b"):
+                missing[(m[2][0] - m[1][0]) % NX].add(name)
+        lacking = {-1: {("P", 0), ("P", 1)}, 1: {("M", 1), ("M", 0)}, -2: {("P", 2), ("M", 2)}}
+        here, held, ready, counted = [0], [], [], {rel: 0 for rel in (0, -1, 1, -2)}
+
+        def multiply(rel, d):
+            counted[rel] += 1
+            rows = pl.ds(pl.multiple_of(block(rel) * ROWS, ROWS), ROWS)
+            deep = pl.ds(pl.multiple_of(lax.rem(x + NX - d, NX) * 512, 512), 512)
+            for w, cols in ((wa, slice(0, CA)), (wb, slice(CA, NP))):
+                r = jnp.dot(u[rows, deep], w[deep, :], preferred_element_type=F32)
+                if counted[rel] > 1:
+                    r = r + pacc[rows, cols]
+                if counted[rel] == NX:
+                    p[rows, cols] = r.astype(BF16)
+                else:
+                    pacc[rows, cols] = r
+
         for name in order:
             if name == "own":
                 for copy in local:
@@ -253,33 +302,24 @@
                     start(other)
             if name in halves:
                 normed(*halves[name])
-
-    def product(n, _):
-        rows = pl.ds(pl.multiple_of(n * 512, 512), 512)
-        p[rows, :CA] = jnp.dot(u[rows, :], wa[...], preferred_element_type=F32).astype(BF16)
-        p[rows, CA:] = jnp.dot(u[rows, :], wb[...], preferred_element_type=F32).astype(BF16)
-        return 0
-
-    with jax.named_scope("project"):
-        lax.fori_loop(0, 2, product, 0)
+            for rel, left in list(lacking.items()):
+                left.discard(name)
+                if not left:
+                    del lacking[rel]
+                    here.append(rel)
+                    ready += [(rel, d) for d in held]
+            for d, left in list(missing.items()):
+                left.discard(name)
+                if not left:
+                    del missing[d]
+                    held.append(d)
+                    ready += [(rel, d) for rel in here]
+            if ready:
+                multiply(*ready.pop(0))
+        for pair in ready:
+            multiply(*pair)
 
     with jax.named_scope("rows"):
-        def picked(v, hit):
-            rows = jnp.broadcast_to(v[...], (8, v.shape[1]))
-            return jnp.dot(rows, hit.astype(F32), precision=HI, preferred_element_type=F32)[:1]
-
-        def two(rows, lanes):
-            return (lax.broadcasted_iota(jnp.int32, (rows, lanes), 0), lax.broadcasted_iota(jnp.int32, (rows, lanes), 1))
-
-        k, c = two(32, 128)
-        of_head = (c >= 64) & (k == 8 * y + lax.shift_right_logical(c - 64, 3))
-        k2, c2 = two(256, 128)
-        bias = picked(dtb, of_head) + picked(lb, (c2 < 64) & (k2 == 64 * y + c2))
-        rates = picked(rate, of_head)
-        k3, c3 = two(32, 512)
-        skips = picked(skip, k3 == 8 * y + lax.shift_right_logical(c3, 6))
-
-        low_tri = (lax.broadcasted_iota(jnp.int32, (ROWS, ROWS), 1) <= lax.broadcasted_iota(jnp.int32, (ROWS, ROWS), 0)).astype(BF16)
         for b in range(4):
             rows = slice(b * ROWS, (b + 1) * ROWS)
             t = softplus(p[rows, MID:].astype(F32) + bias)
@@ -332,10 +372,7 @@
         def state(b):
             rows = slice(b * ROWS, (b + 1) * ROWS)
             tl = jnp.exp(ends[b : b + 1, :] - cu[rows, :]) * td[rows, :]
-            parts = []
-            for h in range(4):
-                parts.append((xf[rows, 128 * h : 128 * h + 128] * halves_of(tl, 64 + 16 * h, 72 + 16 * h, first)).astype(BF16))
-            xt = jnp.concatenate(parts, axis=1)
+            xt = (xf[rows, :] * wide(widened(tl, 8))).astype(BF16)
             return lax.dot_general(bcs[rows, :128], xt, (((0,), (0,)), ((), ())), preferred_element_type=F32)
 
         st = state(0)
@@ -368,22 +405,22 @@
             dt_t = jnp.transpose(td[every, :])
             for r in range(2):
                 rows = pl.ds(pl.multiple_of(base + 128 * r, 128), 128)
-                wide = 128 * (r + 1)
-                seen = pl.ds(base, wide)
+                reach = 128 * (r + 1)
+                seen = pl.ds(base, reach)
                 scores = lax.dot_general(bcs[rows, 128:], bcs[seen, :128], (((1,), (1,)), ((), ())), preferred_element_type=F32)
-                ti, si = two(128, wide)
+                ti, si = two(128, reach)
                 causal = si <= ti + 128 * r
-                cum, lam = cu[rows, :], td[rows, :]
+                cum, lam = cu[rows, :], wide(widened(td[rows, :], 0))
                 for h in range(4):
                     xp = xf[seen, 128 * h : 128 * h + 128].astype(BF16)
                     got = []
                     for e in (2 * h, 2 * h + 1):
                         lane = 64 + 8 * e
-                        differ = jnp.where(causal, cum[:, lane : lane + 1] - cum_t[lane : lane + 1, :wide], -1e30)
-                        w = scores * jnp.exp(differ) * dt_t[lane : lane + 1, :wide]
+                        differ = jnp.where(causal, cum[:, lane : lane + 1] - cum_t[lane : lane + 1, :reach], -1e30)
+                        w = scores * jnp.exp(differ) * dt_t[lane : lane + 1, :reach]
                         got.append(jnp.dot(w.astype(BF16), xp, preferred_element_type=F32))
-                    val = jnp.where(first, got[0], got[1]) * halves_of(lam, 16 * h, 16 * h + 8, first)
                     cols = slice(128 * h, 128 * h + 128)
+                    val = jnp.where(first, got[0], got[1]) * lam[:, cols]
                     yacc[rows, cols] = val + skips[:, cols] * xf[rows, cols]
             return 0
 
@@ -426,9 +463,7 @@
 
         def read(b, rows, bucket, scale, lev):
             r = jnp.dot(bcs[rows, 128:], bucket, preferred_element_type=F32)
-            for h in range(4):
-                cols = slice(128 * h, 128 * h + 128)
-                yacc[rows, cols] += r[:, cols] * halves_of(scale, 16 * h + lev, 16 * h + 8 + lev, first)
+            yacc[rows, :] += r * wide(widened(scale, lev))
 
         def scales(rows, add):
             return pltpu.roll(jnp.exp(cu[rows, :] + add), 64, 1) * td[rows, :]
@@ -471,18 +506,16 @@
                 rows = pl.ds(pl.multiple_of(base + 128 * half, 128), 128)
                 scale = scales(rows, eb[pl.ds(4 + b, 1), :])
                 c = bcs[rows, 128:]
+                pair_of = widened(scale, 0)[0]
                 for h in range(0, 4, 2):
-                    vals = [yacc[rows, 128 * (h + e) : 128 * (h + e) + 128] for e in range(2)]
+                    cols = slice(128 * h, 128 * h + 256)
+                    vals = yacc[rows, cols]
                     for l in range(LEVELS_OUT):
                         pair = [rcv2[l, 8 * (h + e) : 8 * (h + e) + 8].reshape(128, 128) for e in range(2)]
                         r = jnp.dot(c, jnp.concatenate(pair, axis=1), preferred_element_type=F32)
-                        for e in range(2):
-                            lane = 16 * (h + e) + l + 3
-                            vals[e] = vals[e] + r[:, 128 * e : 128 * e + 128] * halves_of(scale, lane, lane + 8, first)
-                    for e in range(2):
-                        cols = slice(128 * (h + e), 128 * (h + e) + 128)
-                        zg = p[rows, 768 + 128 * (h + e) : 896 + 128 * (h + e)].astype(F32)
-                        qs[b, 128 * half : 128 * half + 128, cols] = (vals[e] * jax.nn.silu(zg)).astype(BF16)
+                        vals = vals + r * wide((pair_of, l + 3), cols)
+                    zg = p[rows, 768 + 128 * h : 1024 + 128 * h].astype(F32)
+                    qs[b, 128 * half : 128 * half + 128, cols] = (vals * jax.nn.silu(zg)).astype(BF16)
 
             @pl.when(n < 4)
             def _():
@@ -514,13 +547,10 @@
         for t in range(4):
             cols = slice(512 * t, 512 * t + 512)
             os[t] = (ablk[y, :, cols].astype(F32) + r * acc[:, cols]).astype(BF16)
-            sends.append(remote(os.at[t], oin.at[t], osend.at[t], orecv.at[t], {"section": 1 - s}))
+            sends.append(remote(os.at[t], out.at[:, pl.ds(512 * t, 512)], osend.at[t], orecv.at[t], {"section": 1 - s}))
             sends[-1].start()
-        stores = []
-        for t in range(4):
-            sends[t].wait_recv()
-            stores.append(pltpu.make_async_copy(oin.at[t], out.at[:, pl.ds(512 * t, 512)], dsem.at[t]))
-            stores[-1].start()
+        for copy in sends:
+            copy.wait_recv()
     with jax.named_scope("drain"):
         for name in msgs:
             for copy in copies(name, False):
@@ -538,8 +568,6 @@
             remote(qs.at[0], qr.at[y], qsend.at[n], qrecv.at[n], beside(n)).wait_send()
         for copy in sends:
             copy.wait_send()
-        for copy in stores:
-            copy.wait()
 
 
 def layer(acts, proj, wout, *params):
@@ -557,9 +585,11 @@
             pltpu.VMEM((2048, CB), BF16),
             pltpu.VMEM((NY, ROWS, 2048), BF16),
             pltpu.VMEM((n, 2048), BF16),
+            pltpu.VMEM((n, NP), F32),
             pltpu.VMEM((n, NP), BF16),
             pltpu.VMEM(proj.shape, BF16),
             pltpu.VMEM((NY, 16, 128), BF16),
+            pltpu.VMEM((9, 256, 512), BF16),
             *[pltpu.VMEM(a.shape, a.dtype) for a in params],
             pltpu.VMEM((n + 8, 768), F32),
             pltpu.VMEM((n, 512), F32),
@@ -582,12 +612,11 @@
             pltpu.VMEM((2048, 2048), BF16),
             pltpu.VMEM((ROWS, 2048), F32),
             pltpu.VMEM((4, ROWS, 512), BF16),
-            pltpu.VMEM((4, ROWS, 512), BF16),
             dma((4,)), dma((count,)), dma((count,)), dma((11,)),
-            dma((2,)), dma((2,)), dma((5,)), dma((5,)), dma((2,)), dma((4,)), dma((4,)), dma((4,)), dma((4,)), dma((4,)),
+            dma((2,)), dma((2,)), dma((5,)), dma((5,)), dma((2,)), dma((4,)), dma((4,)), dma((4,)), dma((4,)),
         ],
         compiler_params=pltpu.CompilerParams(
-            collective_id=0, has_side_effects=True, vmem_limit_bytes=62 * 1024 * 1024),
+            collective_id=0, has_side_effects=True, vmem_limit_bytes=56 * 1024 * 1024),
         name="layer",
     )(acts, proj, wout, *params)
 

time: 109 us -> 103 us (0.945)
  Pallas kernels: 107 us -> 100 us
    pallas_call x1, Pallas kernels: 107 us -> 100 us  [layer(): pl.pallas_call(layer_kernel, out_shape=jax.ShapeDtypeStruct((ROWS, 2048),...]
where the time goes in v3:
time: 103 us
  Pallas kernels  100 us (97%)
  local copies, waits for them, and re-layouts  2.3 us (2%)
    pallas_call x1, Pallas kernels, layer(): pl.pallas_call(layer_kernel, out_shape=jax.ShapeDtypeStruct((ROWS, 2048),...  100 us
    unnamed x1, local copies, waits for them, and re-layouts  2.3 us

profile of v3, /device:TPU:3, one launch (start us, length us, event | category | flops | bytes accessed | tf_op | source)
XLA Modules:
  0.0 102.6 jit_solution(5224167760639565299)
XLA Ops:
  0.0 100.3 %layer.1 = bf16[256,2048]{1,0:T(8,128)(2,1)} custom-call(bf16[256,2048]{1,0:T(8,128)(2,1)} %bitcast.7, bf16[16,4640]{1,0:T(8,128)(2,1)} %bitcast.8, bf16[2048,2048]{1,0:T(8,128)(2,1)} %bitcast.5, f32[1,2048]{1,0:T(1,128)} %gain_in.1, f32[4,2304]{1,0:T(4,128)} %bitcast.9, f32[1,2304]{1,0:T(1,128)} %cb_in.1, f32[1,32]{1,0:T(1,128)} %dtb_in.1, ...), custom_call_target="tpu_custom_call" | custom-call | tf_op jit(solution)/shard_map/layer/pallas_call | solution.py:578
  100.3 2.3 %copy.13 = bf16[1,256,2048]{2,1,0:T(8,128)(2,1)} copy(bf16[1,256,2048]{2,1,0:T(8,128)(2,1)} %bitcast.6) | data formatting | bytes 2097152

commit v4 on v3

--- a/solution.py
+++ b/solution.py
@@ -51,52 +51,66 @@
                 dep = (own if d == 0 else ("A1", d)) if k == 1 else ("A2-", d, k - 1)
                 msgs[("A2-", d, k)] = ("a", (-d, k - 1), (0, -1, 0), dep, ua, {"z-": 1})
     offs = [0, -1, 1, -2, 2, -3, 3, -4]
-    for n, o in enumerate(offs):
+    for o in offs:
         dep = own if o == 0 else (("B1+", -o) if o < 0 else ("B1-", o))
         msgs[("B2+", o)] = ("b", (0, o), (1, 0, 0), dep, ub, {"x+": 1})
         msgs[("B2-", o)] = ("b", (0, o), (-1, 0, 0), dep, ub, {"x-": 1})
-        if n in (1, 3, 5):
+        if o in (0, -1, 3, -4):
             msgs[("B2+2", o)] = ("b", (-1, o), (1, 0, 0), ("B2+", o), ub, {"x+": 1})
         else:
             msgs[("B2-2", o)] = ("b", (1, o), (-1, 0, 0), ("B2-", o), ub, {"x-": 1})
     return msgs
 
 
-def schedule(msgs, rate=46.6e3, latency=1.9):
-    free, arrive, order = {}, {}, []
-    started = set()
-    events = []
-
-    def start(name, now):
-        part, chunk, to, dep, size, links = msgs[name]
-        begin = max([now] + [free.get(l, 0.0) for l in links])
-        end = begin
-        for l, n in links.items():
-            free[l] = begin + size * n / rate
-            end = max(end, free[l])
-        arrive[name] = end + latency
-        events.append((end + latency, len(started), name))
-        started.add(name)
-
+BOOST = {(way, d): b for way in ("A2+", "A2-") for d, b in enumerate((0.0, 0.0, -6.0, 0.0))}
+
+
+def schedule(msgs, rate=46.6e3, latency=2.2, early=1.5, window=4.0):
+    kids = {}
     for name, m in msgs.items():
-        if m[3] is None:
-            start(name, 0.0)
-    got = set()
+        kids.setdefault(m[3], []).append(name)
+
+    def path(name):
+        _, _, _, _, size, links = msgs[name]
+        step = size * max(links.values()) / rate + latency
+        return step + max([path(k) for k in kids.get(name, [])], default=0.0)
+
+    def boost(name):
+        return 100.0 if msgs[name][0] == "w" else BOOST.get(name[:2], 0.0) if name[0][:2] == "A2" else 0.0
+
+    rank = {name: -path(name) - boost(name) for name in msgs}
+    free, arrive, events, waiting, plan_of, got = {}, {}, [], [], [], set()
+
+    def issue(now):
+        sent = []
+        for name in sorted(waiting, key=lambda n: (rank[n], str(n))):
+            part, _, _, _, size, links = msgs[name]
+            if part != "w" and any(free.get(l, 0.0) > now + window for l in links):
+                continue
+            begin = max([now] + [free.get(l, 0.0) for l in links])
+            for l, n in links.items():
+                free[l] = begin + size * n / rate
+            arrive[name] = max(free[l] for l in links) + latency + (early if part == "w" else 0.0)
+            events.append((arrive[name], len(arrive), name))
+            sent.append(name)
+        for name in sent:
+            waiting.remove(name)
+        return sent
+
+    waiting += kids[None]
+    first = issue(0.0)
     while events:
         events.sort()
         now, _, name = events.pop(0)
-        order.append(name)
+        waiting += kids.get(name, [])
         got.add(name)
-        if all(("w", d) in got for d in (1, 2, 3)) and "own" not in got:
+        plan_of.append((name, issue(now)))
+        if "own" not in got and all(("w", d) in got for d in (1, 2, 3)):
             got.add("own")
-            order.append("own")
-            for other, m in msgs.items():
-                if m[3] == "own":
-                    start(other, now)
-        for other, m in msgs.items():
-            if m[3] == name:
-                start(other, now)
-    return order, arrive
+            waiting += kids["own"]
+            plan_of.append(("own", issue(now)))
+    assert not waiting
+    return first, plan_of, arrive
 
 
 HI = lax.Precision.HIGHEST
@@ -119,11 +133,11 @@
     return jnp.maximum(v, 0.0) + jnp.log1p(jnp.exp(-jnp.abs(v)))
 
 
-def layer_kernel(acts_in, proj_in, wout_in, gain_in, cw_in, cb_in, dtb_in, rate_in, skip_in, lb_in, gg_in, out,
+def layer_kernel(acts_in, proj_in, wout_in, gain_in, cw_in, cb_in, dtb_in, rate_in, skip_in, lb_in, gg_in, out_low, out_high,
                  wa, wb, ablk, u, pacc, p, proj, small, ones,
                  gain, cw, cb, dtb, rate, skip, lb, gg,
                  ext, xf, bcs, td, cu, yacc, near_st, eb, ee, snd1, slog, rcv1, rlog, table, rcv2, tail,
-                 qs, qr, wout, acc, os,
+                 qs, qr, relay, wout, acc, os,
                  local_sems, send_sems, recv_sems, in_sems,
                  ssem, rsem, lsend, lrecv, tsem, qsend, qrecv, osend, orecv):
     i = lax.axis_index("seq")
@@ -178,7 +192,7 @@
 
         msgs = plan()
         number = {name: n for n, name in enumerate(msgs)}
-        order, _ = schedule(msgs)
+        first_sends, steps, _ = schedule(msgs)
 
         def block(rel):
             return lax.rem(y + rel + 2 * NY, NY)
@@ -208,7 +222,7 @@
             d = to[2]
             rows = pl.ds(pl.multiple_of(seq_of(x, z, y - d) * 16, 16), 16) if arriving else mine
             slot = lax.rem(y + d, NY)
-            return [remote(a, b, send_sems.at[n if e == 0 else len(msgs) + 3 * n + e], recv_sems.at[n if e == 0 else len(msgs) + 3 * n + e], there(*to))
+            return [remote(a, b, send_sems.at[n if e == 0 else len(msgs) + 4 * n + e], recv_sems.at[n if e == 0 else len(msgs) + 4 * n + e], there(*to))
                     for e, (a, b) in enumerate(pieces(slot, rows))]
         if part in ("h0", "h1"):
             ref = ablk.at[block(chunk - back[2]), pl.ds(128 * int(part[1]), 128)]
@@ -232,9 +246,8 @@
         lax.fori_loop(0, 2, step, 0)
 
     with jax.named_scope("gather"):
-        for name, m in msgs.items():
-            if m[3] is None:
-                start(name)
+        for name in first_sends:
+            start(name)
         for copy in loads[2:-1]:
             copy.wait()
         loads[-1].start()
@@ -270,36 +283,42 @@
             return jnp.dot(pair[0], ones[pair[1], :, cols], preferred_element_type=F32)
 
         halves = {("P", 0): (-1, 0), ("P", 1): (-1, 1), ("M", 1): (1, 1), ("M", 0): (1, 0), ("P", 2): (-2, 0), ("M", 2): (2, 1)}
-        missing = {d: set() for d in range(NX)}
+        missing = {(part, d): set() for d in range(NX) for part in "ab"}
         for name, m in msgs.items():
             if m[0] in ("a", "b"):
-                missing[(m[2][0] - m[1][0]) % NX].add(name)
+                missing[(m[0], (m[2][0] - m[1][0]) % NX)].add(name)
         lacking = {-1: {("P", 0), ("P", 1)}, 1: {("M", 1), ("M", 0)}, -2: {("P", 2), ("M", 2)}}
-        here, held, ready, counted = [0], [], [], {rel: 0 for rel in (0, -1, 1, -2)}
-
-        def multiply(rel, d):
-            counted[rel] += 1
-            rows = pl.ds(pl.multiple_of(block(rel) * ROWS, ROWS), ROWS)
+        here, held, ready, counted = [0], [], [], {}
+
+        def multiply():
+            which = ready[0][1]
+            rels = [rel for rel, other in ready if other == which]
+            ready[:] = [e for e in ready if e[1] != which]
+            part, d = which
+            rows = [pl.ds(pl.multiple_of(block(rel) * ROWS, ROWS), ROWS) for rel in rels]
             deep = pl.ds(pl.multiple_of(lax.rem(x + NX - d, NX) * 512, 512), 512)
-            for w, cols in ((wa, slice(0, CA)), (wb, slice(CA, NP))):
-                r = jnp.dot(u[rows, deep], w[deep, :], preferred_element_type=F32)
-                if counted[rel] > 1:
-                    r = r + pacc[rows, cols]
-                if counted[rel] == NX:
-                    p[rows, cols] = r.astype(BF16)
+            w, cols = (wa, slice(0, CA)) if part == "a" else (wb, slice(CA, NP))
+            left = jnp.concatenate([u[r, deep] for r in rows], axis=0)
+            full = jnp.dot(left, w[deep, :], preferred_element_type=F32)
+            for e, (rel, at) in enumerate(zip(rels, rows)):
+                done = counted[rel, part] = counted.get((rel, part), 0) + 1
+                r = full[e * ROWS : (e + 1) * ROWS]
+                if done > 1:
+                    r = r + pacc[at, cols]
+                if done == NX:
+                    p[at, cols] = r.astype(BF16)
                 else:
-                    pacc[rows, cols] = r
-
-        for name in order:
+                    pacc[at, cols] = r
+
+        for name, then in steps:
             if name == "own":
                 for copy in local:
                     copy.wait()
             else:
                 for copy in copies(name, True):
                     copy.wait_recv()
-            for other, m in msgs.items():
-                if m[3] == name:
-                    start(other)
+            for other in then:
+                start(other)
             if name in halves:
                 normed(*halves[name])
             for rel, left in list(lacking.items()):
@@ -315,9 +334,9 @@
                     held.append(d)
                     ready += [(rel, d) for rel in here]
             if ready:
-                multiply(*ready.pop(0))
-        for pair in ready:
-            multiply(*pair)
+                multiply()
+        while ready:
+            multiply()
 
     with jax.named_scope("rows"):
         for b in range(4):
@@ -335,7 +354,7 @@
         eb[4:, :] = jnp.zeros((4, 128), F32)
         ends = eb[...]
         ee[...] = jnp.exp(spread(ends, 512))
-        slog[...] = jnp.broadcast_to(jnp.sum(ends, axis=0, keepdims=True), (8, 128))
+        slog[...] = jnp.sum(ends, axis=0, keepdims=True)
 
     with jax.named_scope("conv"):
         back = remote(p.at[pl.ds(1008, 16), pl.ds(0, 768)], tail, tsem.at[0], tsem.at[1], group(wrap(g + 1)))
@@ -426,6 +445,32 @@
 
         lax.fori_loop(0, 4, inside, 0)
 
+    with jax.named_scope("near"):
+        lane8 = lax.broadcasted_iota(jnp.int32, (1, 128), 1) & 7
+
+        def read(b, rows, bucket, scale, lev):
+            r = jnp.dot(bcs[rows, 128:], bucket, preferred_element_type=F32)
+            yacc[rows, :] += r * wide(widened(scale, lev))
+
+        def scales(rows, add):
+            return pltpu.roll(jnp.exp(cu[rows, :] + add), 64, 1) * td[rows, :]
+
+        zero = jnp.zeros((1, 128), F32)
+        at_block = [pl.ds(b * ROWS, ROWS) for b in range(4)]
+        read(1, at_block[1], near_st[0], scales(at_block[1], zero), 1)
+        read(2, at_block[2], near_st[1], scales(at_block[2], zero), 2)
+        sc = scales(at_block[3], jnp.where(lane8 == 2, ends[2:3, :], 0.0))
+        read(3, at_block[3], near_st[2], sc, 1)
+        read(3, at_block[3], near_st[1], sc, 2)
+
+        def gates(n, _):
+            rows = pl.ds(pl.multiple_of(n * 128, 128), 128)
+            v = p[rows, 768:1280].astype(F32)
+            xf[rows, :] = jax.nn.silu(v)
+            return 0
+
+        lax.fori_loop(0, 8, gates, 0)
+
     with jax.named_scope("wait1"):
         remote(rcv1.at[pl.ds(0, GROUPS - 1)], rcv1.at[pl.ds(0, GROUPS - 1)], ssem.at[0], rsem.at[0], group(g)).wait_recv()
         remote(rlog.at[pl.ds(0, GROUPS - 1)], rlog.at[pl.ds(0, GROUPS - 1)], ssem.at[1], rsem.at[1], group(g)).wait_recv()
@@ -436,46 +481,36 @@
         head_logs = jnp.zeros((GROUPS, 128), F32)
         for n in range(4):
             head_logs = jnp.where(ct == n, wide_logs[:, 128 * n : 128 * n + 128], head_logs)
+        bits = [lax.rem(lax.div(g, 2**l), 2) for l in range(LEVELS_OUT)]
+
+        def give(l):
+            own = lax.div(g, 2 ** (l + 1)) * 2**l + lax.rem(g, 2**l)
+
+            def to_one(k, _):
+                at = lax.rem(own + k, 16)
+                half = lax.div(at, 2**l)
+                to = (2 * half + 1) * 2**l + lax.rem(at, 2**l)
+                src = rcv1.at[2 * half] if l == 0 else table.at[TABLE[l] + half]
+                remote(src, rcv2.at[l, g], lsend.at[l], lrecv.at[l], group(to)).start()
+                return 0
+
+            lax.fori_loop(1, 16, to_one, 0)
+
+            @pl.when(bits[l] == 0)
+            def _():
+                to_one(0, 0)
+
+        give(0)
         level = [rcv1[n].astype(F32) for n in range(GROUPS)]
         ends_of = [head_logs[n : n + 1, :] for n in range(GROUPS)]
-        for l in range(LEVELS_OUT):
+        for l in range(1, LEVELS_OUT):
+            level = [jnp.exp(ends_of[n + 1]) * level[n] + level[n + 1] for n in range(0, len(level), 2)]
+            ends_of = [ends_of[n] + ends_of[n + 1] for n in range(0, len(ends_of), 2)]
             for n in range(0, len(level), 2):
                 table[TABLE[l] + n // 2] = level[n].astype(BF16)
-            level = [jnp.exp(ends_of[n + 1]) * level[n] + level[n + 1] for n in range(0, len(level), 2)]
-            ends_of = [ends_of[n] + ends_of[n + 1] for n in range(0, len(ends_of), 2)]
-
-        def second_send(d, _):
-            to = wrap(g + d)
-            for l in range(LEVELS_OUT):
-                up = lax.div(to, 2**l)
-
-                @pl.when(lax.rem(up, 2) == 1)
-                def _():
-                    remote(table.at[TABLE[l] + lax.div(up, 2)], rcv2.at[l, g], lsend.at[l], lrecv.at[l], group(to)).start()
-
-            return 0
-
-        lax.fori_loop(1, GROUPS, second_send, 0)
-    with jax.named_scope("near"):
-        bits = [lax.rem(lax.div(g, 2**l), 2) for l in range(LEVELS_OUT)]
-
-        lane8 = lax.broadcasted_iota(jnp.int32, (1, 128), 1) & 7
-
-        def read(b, rows, bucket, scale, lev):
-            r = jnp.dot(bcs[rows, 128:], bucket, preferred_element_type=F32)
-            yacc[rows, :] += r * wide(widened(scale, lev))
-
-        def scales(rows, add):
-            return pltpu.roll(jnp.exp(cu[rows, :] + add), 64, 1) * td[rows, :]
-
-        zero = jnp.zeros((1, 128), F32)
-        at_block = [pl.ds(b * ROWS, ROWS) for b in range(4)]
-        read(1, at_block[1], near_st[0], scales(at_block[1], zero), 1)
-        read(2, at_block[2], near_st[1], scales(at_block[2], zero), 2)
-        sc = scales(at_block[3], jnp.where(lane8 == 2, ends[2:3, :], 0.0))
-        read(3, at_block[3], near_st[2], sc, 1)
-        read(3, at_block[3], near_st[1], sc, 2)
-
+            give(l)
+
+    with jax.named_scope("outer"):
         row_of = lax.broadcasted_iota(jnp.int32, (GROUPS, 1), 0)
         outer = zero
         for l in range(LEVELS_OUT):
@@ -488,51 +523,84 @@
             run = run + ends[b : b + 1, :]
 
     with jax.named_scope("wait2"):
+        def bucket(l, h):
+            return jnp.concatenate([rcv2[l, 8 * e : 8 * e + 8].reshape(128, 128) for e in (h, h + 1)], axis=1)
+
+        def scaled(n):
+            rows = pl.ds(pl.multiple_of(n * 128, 128), 128)
+            return rows, widened(scales(rows, eb[pl.ds(4 + lax.div(n, 2), 1), :]), 0)[0], bcs[rows, 128:]
+
         for l in range(LEVELS_OUT):
             @pl.when(bits[l] == 1)
             def _():
                 remote(rcv2.at[l, pl.ds(0, GROUPS - 1)], rcv2.at[l, pl.ds(0, GROUPS - 1)], lsend.at[l], lrecv.at[l], group(g)).wait_recv()
-                rcv2[l, g] = table[TABLE[l] + lax.div(g, 2 ** (l + 1))]
-
-            @pl.when(bits[l] == 0)
-            def _():
-                rcv2[l] = jnp.zeros((GROUPS, 16, 128), BF16)
+                rcv2[l, g] = rcv1[2 * lax.div(g, 2)] if l == 0 else table[TABLE[l] + lax.div(g, 2 ** (l + 1))]
+
+            if l < LEVELS_OUT - 1:
+                @pl.when(bits[l] == 1)
+                def _():
+                    def add(n, _):
+                        rows, pair_of, c = scaled(n)
+                        for h in (0, 2):
+                            cols = slice(128 * h, 128 * h + 256)
+                            r = jnp.dot(c, bucket(l, h), preferred_element_type=F32)
+                            yacc[rows, cols] += r * wide((pair_of, l + 3), cols)
+                        return 0
+
+                    lax.fori_loop(0, 8, add, 0)
 
     with jax.named_scope("finish"):
-        def finish(n, _):
-            b = lax.rem(y + n, NY)
-            base = pl.multiple_of(b * ROWS, ROWS)
+        last = LEVELS_OUT - 1
+
+        @pl.when(bits[last] == 0)
+        def _():
+            rcv2[last] = jnp.zeros((GROUPS, 16, 128), BF16)
+
+        def finish(b):
             for half in range(2):
-                rows = pl.ds(pl.multiple_of(base + 128 * half, 128), 128)
-                scale = scales(rows, eb[pl.ds(4 + b, 1), :])
-                c = bcs[rows, 128:]
-                pair_of = widened(scale, 0)[0]
-                for h in range(0, 4, 2):
+                rows, pair_of, c = scaled(2 * b + half)
+                for h in (0, 2):
                     cols = slice(128 * h, 128 * h + 256)
-                    vals = yacc[rows, cols]
-                    for l in range(LEVELS_OUT):
-                        pair = [rcv2[l, 8 * (h + e) : 8 * (h + e) + 8].reshape(128, 128) for e in range(2)]
-                        r = jnp.dot(c, jnp.concatenate(pair, axis=1), preferred_element_type=F32)
-                        vals = vals + r * wide((pair_of, l + 3), cols)
-                    zg = p[rows, 768 + 128 * h : 1024 + 128 * h].astype(F32)
-                    qs[b, 128 * half : 128 * half + 128, cols] = (vals * jax.nn.silu(zg)).astype(BF16)
-
-            @pl.when(n < 4)
-            def _():
-                remote(qs.at[b], qr.at[y], qsend.at[n], qrecv.at[n], beside(n)).start()
-
-            return 0
-
-        lax.fori_loop(1, 5, finish, 0)
+                    r = jnp.dot(c, bucket(last, h), preferred_element_type=F32)
+                    vals = yacc[rows, cols] + r * wide((pair_of, last + 3), cols)
+                    qs[b, 128 * half : 128 * half + 128, cols] = (vals * xf[rows, cols]).astype(BF16)
+
+        def side(n):
+            return lax.rem(y + n, NY)
+
+        lower, upper = pl.ds(0, 128), pl.ds(128, 128)
+        first_hop = [remote(qs.at[side(2), lower], relay.at[0], qsend.at[0], qrecv.at[0], beside(1)),
+                     remote(qs.at[side(2), upper], relay.at[1], qsend.at[1], qrecv.at[1], beside(3))]
+        next_hop = [remote(relay.at[0], qr.at[side(3), lower], qsend.at[2], qrecv.at[2], beside(1)),
+                    remote(relay.at[1], qr.at[side(1), upper], qsend.at[3], qrecv.at[3], beside(3))]
+        direct = [remote(qs.at[side(1)], qr.at[y], qsend.at[4], qrecv.at[4], beside(1)),
+                  remote(qs.at[side(3)], qr.at[y], qsend.at[5], qrecv.at[5], beside(3))]
+        finish(side(2))
+        for copy in first_hop:
+            copy.start()
+        finish(side(1))
+        direct[0].start()
+        finish(side(3))
+        direct[1].start()
+        finish(y)
+        for a, b in zip(first_hop, next_hop):
+            a.wait_recv()
+            b.start()
     with jax.named_scope("out"):
         qr[y] = qs[y]
         loads[-1].wait()
 
         squares = jnp.zeros((ROWS, 1), F32)
+        sends = []
         for at, n in enumerate((0, 1, 3, 2)):
             src = lax.rem(y + NY - n, NY)
-            if n:
-                remote(qs.at[0], qr.at[src], qsend.at[n], qrecv.at[n], beside(n)).wait_recv()
+            if n == 1:
+                direct[0].wait_recv()
+            elif n == 3:
+                direct[1].wait_recv()
+            elif n == 2:
+                for copy in next_hop:
+                    copy.wait_recv()
             v = qr[src].astype(F32)
             squares = squares + jnp.sum(v * v, axis=1, keepdims=True)
             lanes = pl.ds(pl.multiple_of(src * 512, 512), 512)
@@ -540,15 +608,14 @@
             for t in range(4):
                 cols = slice(512 * t, 512 * t + 512)
                 part = jnp.dot(v, wout[lanes, cols], preferred_element_type=F32)
-                acc[:, cols] = part if at == 0 else acc[:, cols] + part
+                if at < 3:
+                    acc[:, cols] = part if at == 0 else acc[:, cols] + part
+                    continue
+                r = lax.rsqrt(squares * (1.0 / 2048.0) + EPS)
+                os[t] = (ablk[y, :, cols].astype(F32) + r * (acc[:, cols] + part)).astype(BF16)
+                sends.append(remote(os.at[t], (out_low, out_high)[t // 2].at[:, pl.ds(512 * (t % 2), 512)], osend.at[t], orecv.at[t], {"section": 1 - s}))
+                sends[-1].start()
     with jax.named_scope("swap"):
-        r = lax.rsqrt(squares * (1.0 / 2048.0) + EPS)
-        sends = []
-        for t in range(4):
-            cols = slice(512 * t, 512 * t + 512)
-            os[t] = (ablk[y, :, cols].astype(F32) + r * acc[:, cols]).astype(BF16)
-            sends.append(remote(os.at[t], out.at[:, pl.ds(512 * t, 512)], osend.at[t], orecv.at[t], {"section": 1 - s}))
-            sends[-1].start()
         for copy in sends:
             copy.wait_recv()
     with jax.named_scope("drain"):
@@ -564,8 +631,8 @@
                 def _():
                     some = rcv2.at[l, pl.ds(0, 16 - bit)]
                     remote(some, some, lsend.at[l], lrecv.at[l], group(g)).wait_send()
-        for n in (1, 2, 3):
-            remote(qs.at[0], qr.at[y], qsend.at[n], qrecv.at[n], beside(n)).wait_send()
+        for copy in first_hop + next_hop + direct:
+            copy.wait_send()
         for copy in sends:
             copy.wait_send()
 
@@ -573,13 +640,13 @@
 def layer(acts, proj, wout, *params):
     anywhere = pl.BlockSpec(memory_space=pl.ANY)
     n = NY * ROWS
-    count = 4 * len(plan())
+    count = 2 * len(plan())
     dma = pltpu.SemaphoreType.DMA
     return pl.pallas_call(
         layer_kernel,
-        out_shape=jax.ShapeDtypeStruct((ROWS, 2048), BF16),
+        out_shape=[jax.ShapeDtypeStruct((ROWS, 1024), BF16)] * 2,
         in_specs=[anywhere] * (3 + len(params)),
-        out_specs=anywhere,
+        out_specs=[anywhere] * 2,
         scratch_shapes=[
             pltpu.VMEM((2048, CA), BF16),
             pltpu.VMEM((2048, CB), BF16),
@@ -601,29 +668,30 @@
             pltpu.VMEM((8, 128), F32),
             pltpu.VMEM((8, 512), F32),
             pltpu.VMEM((GROUPS, 16, 128), BF16),
-            pltpu.VMEM((8, 128), F32),
+            pltpu.VMEM((1, 128), F32),
             pltpu.VMEM((GROUPS, 16, 128), BF16),
-            pltpu.VMEM((GROUPS, 8, 128), F32),
+            pltpu.VMEM((GROUPS, 1, 128), F32),
             pltpu.VMEM((31, 16, 128), BF16),
             pltpu.VMEM((LEVELS_OUT, GROUPS, 16, 128), BF16),
             pltpu.VMEM((16, 768), BF16),
             pltpu.VMEM((NY, ROWS, 512), BF16),
             pltpu.VMEM((NY, ROWS, 512), BF16),
+            pltpu.VMEM((2, 128, 512), BF16),
             pltpu.VMEM((2048, 2048), BF16),
             pltpu.VMEM((ROWS, 2048), F32),
             pltpu.VMEM((4, ROWS, 512), BF16),
-            dma((4,)), dma((count,)), dma((count,)), dma((11,)),
-            dma((2,)), dma((2,)), dma((5,)), dma((5,)), dma((2,)), dma((4,)), dma((4,)), dma((4,)), dma((4,)),
+            dma((5,)), dma((count,)), dma((count,)), dma((11,)),
+            dma((2,)), dma((2,)), dma((5,)), dma((5,)), dma((2,)), dma((6,)), dma((6,)), dma((4,)), dma((4,)),
         ],
         compiler_params=pltpu.CompilerParams(
-            collective_id=0, has_side_effects=True, vmem_limit_bytes=56 * 1024 * 1024),
+            collective_id=0, has_side_effects=True, vmem_limit_bytes=58 * 1024 * 1024),
         name="layer",
     )(acts, proj, wout, *params)
 
 
 def per_device(acts, in_proj, out_proj, conv_weight, conv_bias, dt_bias, decay_rate, skip_gain, level_bias, norm_gain, gate_gain):
-    o = layer(acts[0], in_proj[0], out_proj[0], norm_gain, conv_weight[0], conv_bias, dt_bias, decay_rate, skip_gain, level_bias, gate_gain)
-    return o[None]
+    low, high = layer(acts[0], in_proj[0], out_proj[0], norm_gain, conv_weight[0], conv_bias, dt_bias, decay_rate, skip_gain, level_bias, gate_gain)
+    return jnp.concatenate([low, high], axis=1)[None]
 
 
 def solution(mesh):

time: 103 us -> 97.5 us (0.947)
  Pallas kernels: 100 us -> 95.1 us
  local copies, waits for them, and re-layouts: 2.3 us -> 0 us
  other arithmetic: 0 us -> 2.27 us
    pallas_call x1, Pallas kernels: 100 us -> 95.1 us  [layer(): pl.pallas_call(layer_kernel, out_shape=[jax.ShapeDtypeStruct((ROWS, 1024)...]
    unnamed x1 -> x0, local copies, waits for them, and re-layouts: 2.3 us -> none
    broadcast_in_dim x0 -> x1, other arithmetic: none -> 2.27 us  [per_device(): return jnp.concatenate([low, high], axis=1)[None]]
where the time goes in v4:
time: 97.5 us; the launch traced here: 97.4 us
  Pallas kernels  95.1 us (98%)
  other arithmetic  2.27 us (2%)
    pallas_call x1, Pallas kernels, layer(): pl.pallas_call(layer_kernel, out_shape=[jax.ShapeDtypeStruct((ROWS, 1024)...  95.1 us
    broadcast_in_dim x1, other arithmetic, per_device(): return jnp.concatenate([low, high], axis=1)[None]  2.27 us

profile of v4, /device:TPU:3, one launch (start us, length us, event | category | flops | bytes accessed | tf_op | source)
XLA Modules:
  0.0 97.4 jit_solution(13177666512518588709)
XLA Ops:
  0.0 95.1 %layer.1 = (bf16[256,1024]{1,0:T(8,128)(2,1)}, bf16[256,1024]{1,0:T(8,128)(2,1)}) custom-call(bf16[256,2048]{1,0:T(8,128)(2,1)} %bitcast.7, bf16[16,4640]{1,0:T(8,128)(2,1)} %bitcast.8, bf16[2048,2048]{1,0:T(8,128)(2,1)} %bitcast.6, f32[1,2048]{1,0:T(1,128)} %gain_in.1, f32[4,2304]{1,0:T(4,128)} %bitcast.9, f32[1,2304]{1,0:T(1,128)} %cb_in.1, ...), custom_call_target="tpu_custom_call" | custom-call | tf_op jit(solution)/shard_map/layer/pallas_call | solution.py:645
  95.1 2.3 %maximum_bitcast_fusion = bf16[1,256,2048]{2,1,0:T(8,128)(2,1)} fusion(bf16[256,1024]{1,0:T(8,128)(2,1)} %get-tuple-element.8, bf16[256,1024]{1,0:T(8,128)(2,1)} %get-tuple-element.7), kind=kLoop, calls=%fused_computation | loop fusion | flops 2097152 | bytes 2097152 | tf_op jit(solution)/shard_map/broadcast_in_dim | solution.py:694

commit v5 on v4

--- a/solution.py
+++ b/solution.py
@@ -166,13 +166,9 @@
     with jax.named_scope("enter"):
         barrier = pltpu.get_barrier_semaphore()
 
-        def greet(d, _):
-            pl.semaphore_signal(barrier, inc=1, device_id=group(wrap(g + d)), device_id_type=MESH)
-            return 0
-
-        lax.fori_loop(1, GROUPS, greet, 0)
-        for d in (1, 2, 3):
-            pl.semaphore_signal(barrier, inc=1, device_id=beside(d), device_id_type=MESH)
+        near = ((1, 0, 0), (-1, 0, 0), (2, 0, 0), (0, 1, 0), (0, -1, 0), (0, 0, 1), (0, 0, -1), (0, 0, 2))
+        for to in near:
+            pl.semaphore_signal(barrier, inc=1, device_id=there(*to), device_id_type=MESH)
         pl.semaphore_signal(barrier, inc=1, device_id={"section": 1 - s}, device_id_type=MESH)
         pairs = ((proj_in, proj), (acts_in, ablk.at[y]), (gain_in, gain), (cw_in, cw), (cb_in, cb), (dtb_in, dtb),
                  (rate_in, rate), (skip_in, skip), (lb_in, lb), (gg_in, gg), (wout_in, wout))
@@ -212,7 +208,7 @@
         for copy in local:
             copy.start()
         loads[1].wait()
-        pl.semaphore_wait(barrier, GROUPS - 1 + 3 + 1)
+        pl.semaphore_wait(barrier, len(near) + 1)
 
     def copies(name, arriving):
         part, chunk, to, dep, _, _ = msgs[name]

time: 97.5 us -> 95.5 us (0.979)
  Pallas kernels: 95.1 us -> 92.4 us
    pallas_call x1, Pallas kernels: 95.1 us -> 92.4 us  [layer(): pl.pallas_call(layer_kernel, out_shape=[jax.ShapeDtypeStruct((ROWS, 1024)...]
where the time goes in v5:
time: 95.5 us; the launch traced here: 94.7 us
  Pallas kernels  92.4 us (97%)
  other arithmetic  2.27 us (2%)
    pallas_call x1, Pallas kernels, layer(): pl.pallas_call(layer_kernel, out_shape=[jax.ShapeDtypeStruct((ROWS, 1024)...  92.4 us
    broadcast_in_dim x1, other arithmetic, per_device(): return jnp.concatenate([low, high], axis=1)[None]  2.27 us

profile of v5, /device:TPU:3, one launch (start us, length us, event | category | flops | bytes accessed | tf_op | source)
XLA Modules:
  0.0 94.7 jit_solution(830165167465003012)
XLA Ops:
  0.0 92.4 %layer.1 = (bf16[256,1024]{1,0:T(8,128)(2,1)}, bf16[256,1024]{1,0:T(8,128)(2,1)}) custom-call(bf16[256,2048]{1,0:T(8,128)(2,1)} %bitcast.7, bf16[16,4640]{1,0:T(8,128)(2,1)} %bitcast.8, bf16[2048,2048]{1,0:T(8,128)(2,1)} %bitcast.6, f32[1,2048]{1,0:T(1,128)} %gain_in.1, f32[4,2304]{1,0:T(4,128)} %bitcast.9, f32[1,2304]{1,0:T(1,128)} %cb_in.1, ...), custom_call_target="tpu_custom_call" | custom-call | tf_op jit(solution)/shard_map/layer/pallas_call | solution.py:641
  92.4 2.3 %maximum_bitcast_fusion = bf16[1,256,2048]{2,1,0:T(8,128)(2,1)} fusion(bf16[256,1024]{1,0:T(8,128)(2,1)} %get-tuple-element.8, bf16[256,1024]{1,0:T(8,128)(2,1)} %get-tuple-element.7), kind=kLoop, calls=%fused_computation | loop fusion | flops 2097152 | bytes 2097152 | tf_op jit(solution)/shard_map/broadcast_in_dim | solution.py:690

commit v6 on v5

--- a/solution.py
+++ b/solution.py
@@ -609,8 +609,10 @@
                     continue
                 r = lax.rsqrt(squares * (1.0 / 2048.0) + EPS)
                 os[t] = (ablk[y, :, cols].astype(F32) + r * (acc[:, cols] + part)).astype(BF16)
-                sends.append(remote(os.at[t], (out_low, out_high)[t // 2].at[:, pl.ds(512 * (t % 2), 512)], osend.at[t], orecv.at[t], {"section": 1 - s}))
-                sends[-1].start()
+                for half, to in enumerate((out_low, out_high)):
+                    n_send = 2 * t + half
+                    sends.append(remote(os.at[t, pl.ds(128 * half, 128)], to.at[:, pl.ds(512 * t, 512)], osend.at[n_send], orecv.at[n_send], {"section": 1 - s}))
+                    sends[-1].start()
     with jax.named_scope("swap"):
         for copy in sends:
             copy.wait_recv()
@@ -640,7 +642,7 @@
     dma = pltpu.SemaphoreType.DMA
     return pl.pallas_call(
         layer_kernel,
-        out_shape=[jax.ShapeDtypeStruct((ROWS, 1024), BF16)] * 2,
+        out_shape=[jax.ShapeDtypeStruct((ROWS // 2, 2048), BF16)] * 2,
         in_specs=[anywhere] * (3 + len(params)),
         out_specs=[anywhere] * 2,
         scratch_shapes=[
@@ -677,7 +679,7 @@
             pltpu.VMEM((ROWS, 2048), F32),
             pltpu.VMEM((4, ROWS, 512), BF16),
             dma((5,)), dma((count,)), dma((count,)), dma((11,)),
-            dma((2,)), dma((2,)), dma((5,)), dma((5,)), dma((2,)), dma((6,)), dma((6,)), dma((4,)), dma((4,)),
+            dma((2,)), dma((2,)), dma((5,)), dma((5,)), dma((2,)), dma((6,)), dma((6,)), dma((8,)), dma((8,)),
         ],
         compiler_params=pltpu.CompilerParams(
             collective_id=0, has_side_effects=True, vmem_limit_bytes=58 * 1024 * 1024),
@@ -687,7 +689,7 @@
 
 def per_device(acts, in_proj, out_proj, conv_weight, conv_bias, dt_bias, decay_rate, skip_gain, level_bias, norm_gain, gate_gain):
     low, high = layer(acts[0], in_proj[0], out_proj[0], norm_gain, conv_weight[0], conv_bias, dt_bias, decay_rate, skip_gain, level_bias, gate_gain)
-    return jnp.concatenate([low, high], axis=1)[None]
+    return jnp.concatenate([low, high], axis=0)[None]
 
 
 def solution(mesh):

time: 95.5 us -> 95.6 us (level)
  no operation moved by 1% of the time
where the time goes in v6:
time: 95.6 us; the launch traced here: 94.8 us
  Pallas kernels  92.5 us (97%)
  other arithmetic  2.28 us (2%)
    pallas_call x1, Pallas kernels, layer(): pl.pallas_call(layer_kernel, out_shape=[jax.ShapeDtypeStruct((ROWS // 2,...  92.5 us
    broadcast_in_dim x1, other arithmetic, per_device(): return jnp.concatenate([low, high], axis=0)[None]  2.28 us

profile of v6, /device:TPU:3, one launch (start us, length us, event | category | flops | bytes accessed | tf_op | source)
XLA Modules:
  0.0 94.8 jit_solution(12594953606933739838)
XLA Ops:
  0.0 92.5 %layer.1 = (bf16[128,2048]{1,0:T(8,128)(2,1)}, bf16[128,2048]{1,0:T(8,128)(2,1)}) custom-call(bf16[256,2048]{1,0:T(8,128)(2,1)} %bitcast.7, bf16[16,4640]{1,0:T(8,128)(2,1)} %bitcast.8, bf16[2048,2048]{1,0:T(8,128)(2,1)} %bitcast.6, f32[1,2048]{1,0:T(1,128)} %gain_in.1, f32[4,2304]{1,0:T(4,128)} %bitcast.9, f32[1,2304]{1,0:T(1,128)} %cb_in.1, ...), custom_call_target="tpu_custom_call" | custom-call | tf_op jit(solution)/shard_map/layer/pallas_call | solution.py:643
  92.5 2.3 %maximum_bitcast_fusion = bf16[1,256,2048]{2,1,0:T(8,128)(2,1)} fusion(bf16[128,2048]{1,0:T(8,128)(2,1)} %get-tuple-element.8, bf16[128,2048]{1,0:T(8,128)(2,1)} %get-tuple-element.7), kind=kLoop, calls=%fused_computation | loop fusion | flops 2097152 | bytes 2097152 | tf_op jit(solution)/shard_map/broadcast_in_dim | solution.py:692
